TPU v7x, 32 devices: a whole 2x2x4 slice. The times are simulated.
32 devices in a mesh: batch: 8 (over z, x), mp: 4 (over y, core).
Axes of the slice: x: 2, y: 2, z: 4, core: 2. Of those that a mesh axis runs over, the one named last changes fastest.
Arguments:
- features: bfloat16 [1024, 65536], P('batch', 'mp'), may hold values from 0 to 4
- tiles: bfloat16 [2, 512, 3, 128, 128], P(None, 'mp', None, 'batch'), may hold values from -0.3125 to 0.3125
- biases: float32 [2, 65536], P(None, 'mp'), may hold values from -0.5 to 0
- in_block: int32 [2, 512, 3], replicated, may hold values from 0 to 511, as said below
Outputs:
- activations: bfloat16 [1024, 65536], P('batch', 'mp')
- row_means: float32 [1024], P('batch')
- grand: float32 [], replicated
Inputs may be any that keep to these rules, and one draw needn't show every extreme that they name: `in_block`: number the 384 tiles of mp shard m (column blocks m * 128 to (m + 1) * 128 - 1) in order of column block, then tile slot; tile number s reads a block of shard s // 96, that is an id in [(s // 96) * 128, (s // 96 + 1) * 128).
All inputs are finite; a program needn't handle non-finite values.
Results may differ from a plain program's by a relative error of at most 0.0052.
Values may be sent and summed in bfloat16 or wider, within the bound.
A program may use at most 128 MiB of HBM per device.

v0:
```python
import functools
import math

import jax
import jax.numpy as jnp
from jax import lax
from jax.experimental import pallas as pl
from jax.experimental.pallas import tpu as pltpu
from jax.sharding import PartitionSpec as P

MESH = pl.DeviceIdType.MESH


def geometry(mesh):
    groups, shards = mesh.devices.shape
    where = [getattr(d, "coords", None) for d in mesh.devices[:, 0]]
    if groups == 1 or where[0] is None or where[0] == where[1]:
        return groups, 1, True, 1
    moved = [i for i in range(len(where[0])) if where[0][i] != where[1][i]][0]
    minor = 1
    while minor < groups and all(
        where[minor][i] == where[0][i] for i in range(len(where[0])) if i != moved
    ):
        minor += 1
    major = groups // minor
    row = [d.coords for d in mesh.devices[0, :]]
    cores = sum(1 for c in row if c == row[0])
    if major >= minor:
        return major, minor, True, cores
    return minor, major, False, cores


def gather_kernel(
    geo, shards, layer, pieces,
    tiles, cur, wout, xout,
    wv, xv, lsem, wrecv, wup, wdn, wcross, whalf, xrecv, xfar, xcore,
):
    nl, nq, line_major, nc = geo
    ny = shards // nc
    bi = lax.axis_index("batch")
    mi = lax.axis_index("mp")
    if line_major:
        l, q = bi // nq, bi % nq
    else:
        l, q = bi % nl, bi // nl
    y, core = mi // nc, mi % nc
    step_w = tiles.shape[1] // pieces
    step_x = cur.shape[0] // pieces
    halves = nq == 2 and nl % 2 == 0
    first = pieces // 2

    def group(level, side):
        return level * nq + side if line_major else side * nl + level

    sides = [(q + d) % nq for d in range(1, nq)]
    fars = [((y + d) % ny) * nc + core for d in range(1, ny)]
    partners = [y * nc + (core + d) % nc for d in range(1, nc)]

    barrier = pltpu.get_barrier_semaphore()

    def greet(b, m):
        pl.semaphore_signal(barrier, inc=1, device_id=(b, m), device_id_type=MESH)

    @pl.when(l > 0)
    def _():
        greet(group(l - 1, q), mi)

    @pl.when(l < nl - 1)
    def _():
        greet(group(l + 1, q), mi)

    for side in sides:
        greet(group(l, side), mi)
    for m in fars + partners:
        greet(bi, m)
    near = jnp.where(l > 0, 1, 0) + jnp.where(l < nl - 1, 1, 0)
    pl.semaphore_wait(barrier, len(sides) + len(fars) + len(partners) + near)

    in_w = pltpu.make_async_copy(tiles.at[layer], wv, lsem.at[0])
    in_x = pltpu.make_async_copy(cur, xv, lsem.at[1])
    in_w.start()
    in_x.start()

    def wcopy(own, b, c, to, ssem):
        part = pl.ds(c * step_w, step_w)
        return pltpu.make_async_remote_copy(
            src_ref=tiles.at[layer, part] if own else wout.at[b, part],
            dst_ref=wout.at[b, part],
            send_sem=ssem,
            recv_sem=wrecv.at[b, c],
            device_id=(to, mi),
            device_id_type=MESH,
        )

    def xcopy(own, m, c, to, ssem):
        part = pl.ds(c * step_x, step_x)
        return pltpu.make_async_remote_copy(
            src_ref=cur.at[part] if own else xout.at[m, part],
            dst_ref=xout.at[m, part],
            send_sem=ssem,
            recv_sem=xrecv.at[m, c],
            device_id=(bi, to),
            device_id_type=MESH,
        )

    def phase(p, c, drain):
        def go(copy):
            copy.wait_send() if drain else copy.start()

        def arrived_w(b):
            if not drain:
                wcopy(False, b, c, bi, wup.at[0, c]).wait_recv()

        if p == 0:
            @pl.when(l < nl - 1)
            def _():
                go(wcopy(True, bi, c, group(l + 1, q), wup.at[0, c]))

            @pl.when(l > 0)
            def _():
                go(wcopy(True, bi, c, group(l - 1, q), wdn.at[0, c]))

            for i, side in enumerate(sides):
                go(wcopy(True, bi, c, group(l, side), wcross.at[i, l, c]))
            for i, m in enumerate(fars):
                go(xcopy(True, mi, c, m, xfar.at[i, c]))
            for i, m in enumerate(partners):
                go(xcopy(True, mi, c, m, xcore.at[i, y, c]))
        else:
            @pl.when(l - p >= 0)
            def _():
                b = group(l - p, q)
                arrived_w(b)

                @pl.when(l < nl - 1)
                def _():
                    go(wcopy(False, b, c, group(l + 1, q), wup.at[p, c]))

                def across():
                    for i, side in enumerate(sides):
                        go(wcopy(False, b, c, group(l, side), wcross.at[i, l - p, c]))

                if halves and p == 1:
                    pl.when((l < nl // 2) | (c < first))(across)
                else:
                    across()

            @pl.when(l + p <= nl - 1)
            def _():
                b = group(l + p, q)
                arrived_w(b)

                @pl.when(l > 0)
                def _():
                    go(wcopy(False, b, c, group(l - 1, q), wdn.at[p, c]))

                def across():
                    for i, side in enumerate(sides):
                        go(wcopy(False, b, c, group(l, side), wcross.at[i, l + p, c]))

                if halves and p == 1:
                    pl.when((l >= nl // 2) | (c < first))(across)
                else:
                    across()

            if halves and p == 1:
                @pl.when(c >= first)
                def _():
                    b = group(l, sides[0])
                    arrived_w(b)

                    @pl.when((l + 1 >= nl // 2) & (l < nl - 1))
                    def _():
                        go(wcopy(False, b, c, group(l + 1, q), whalf.at[0, c]))

                    @pl.when((l - 1 < nl // 2) & (l > 0))
                    def _():
                        go(wcopy(False, b, c, group(l - 1, q), whalf.at[1, c]))

        if p == nl - 1:
            for d, far in enumerate(fars):
                if not drain:
                    xcopy(False, far, c, mi, xfar.at[0, c]).wait_recv()
                for i, m in enumerate(partners):
                    go(xcopy(False, far, c, m, xcore.at[i, far // nc, c]))

    for p in range(nl):
        @pl.loop(0, pieces)
        def _(c, p=p):
            phase(p, c, False)

        if p == 0:
            in_w.wait()
            in_x.wait()
            out_w = pltpu.make_async_copy(wv, wout.at[bi], lsem.at[2])
            out_x = pltpu.make_async_copy(xv, xout.at[mi], lsem.at[3])
            out_w.start()
            out_x.start()

    @pl.loop(0, pieces)
    def _(c):
        for side in sides:
            for level in range(nl):
                b = group(level, side)

                def arrive(b=b):
                    wcopy(False, b, c, bi, wup.at[0, c]).wait_recv()

                if halves:
                    pl.when((l != level) | (c < first))(arrive)
                else:
                    arrive()
        for m in partners:
            for yy in range(ny):
                xcopy(False, yy * nc + m % nc, c, mi, xfar.at[0, c]).wait_recv()

    out_w.wait()
    out_x.wait()
    for p in range(nl):
        @pl.loop(0, pieces)
        def _(c, p=p):
            phase(p, c, True)


def gather(geo, shards, groups, layer, tiles, cur):
    nl, nq, _, nc = geo
    pieces = 8 if groups <= 8 else 2
    ny = shards // nc
    dma = pltpu.SemaphoreType.DMA
    return pl.pallas_call(
        functools.partial(gather_kernel, geo, shards, layer, pieces),
        out_shape=(
            jax.ShapeDtypeStruct((groups,) + tiles.shape[1:], tiles.dtype),
            jax.ShapeDtypeStruct((shards,) + cur.shape, cur.dtype),
        ),
        in_specs=[pl.BlockSpec(memory_space=pl.ANY)] * 2,
        out_specs=(pl.BlockSpec(memory_space=pl.ANY),) * 2,
        scratch_shapes=[
            pltpu.VMEM(tiles.shape[1:], tiles.dtype),
            pltpu.VMEM(cur.shape, cur.dtype),
            dma((4,)),
            dma((groups, pieces)),
            dma((nl, pieces)),
            dma((nl, pieces)),
            dma((max(nq - 1, 1), nl, pieces)),
            dma((2, pieces)),
            dma((shards, pieces)),
            dma((max(ny - 1, 1), pieces)),
            dma((max(nc - 1, 1), ny, pieces)),
        ],
        compiler_params=pltpu.CompilerParams(collective_id=layer, has_side_effects=True),
        name=f"gather_{layer}",
    )(tiles, cur)


def layer_kernel(ids, x_ref, w_ref, b_ref, o_ref, r_ref, xl, wl, s_ref, loads):
    shards, rows, _ = x_ref.shape
    _, cb, fan, _, side = w_ref.shape
    per_shard = cb // shards
    width = math.gcd(per_shard, 8)

    def pulls(s):
        part = pl.ds(s * per_shard, per_shard)
        return (
            pltpu.make_async_copy(x_ref.at[s], xl.at[s], loads.at[0, s]),
            pltpu.make_async_copy(w_ref.at[:, part], wl.at[:, part], loads.at[1, s]),
        )

    for s in range(min(2, shards)):
        for pull in pulls(s):
            pull.start()
    s_ref[...] = jnp.zeros_like(s_ref)
    for s in range(shards):
        for pull in pulls(s):
            pull.wait()
        if s + 2 < shards:
            for pull in pulls(s + 2):
                pull.start()

        @pl.loop(0, per_shard // width)
        def _(k, s=s):
            for jj in range(width):
                j = s * per_shard + k * width + jj
                xs, ws = [], []
                for t in range(fan):
                    at = ids[j * fan + t]
                    xs.append(xl[s, :, pl.ds(pl.multiple_of(at * side, side), side)])
                    ws.append(wl[:, j, t].reshape(side, side))
                total = jnp.dot(
                    jnp.concatenate(xs, axis=1),
                    jnp.concatenate(ws, axis=0),
                    preferred_element_type=jnp.float32,
                )
                cols = pl.ds(pl.multiple_of(j * side, side), side)
                out = jnp.clip(total + b_ref[:, cols], 0.0, 32.0).astype(o_ref.dtype)
                o_ref[:, cols] = out
                s_ref[...] += out.astype(jnp.float32)

    line = jnp.sum(s_ref[...].T, axis=0, keepdims=True)
    r_ref[...] = jnp.broadcast_to(line, r_ref.shape)


def apply_layer(ids, xall, wall, bias):
    shards, rows, width = xall.shape
    side = wall.shape[4]
    hbm = pl.BlockSpec(memory_space=pl.ANY)
    vmem = pl.BlockSpec(memory_space=pltpu.VMEM)
    return pl.pallas_call(
        layer_kernel,
        out_shape=(
            jax.ShapeDtypeStruct((rows, width), xall.dtype),
            jax.ShapeDtypeStruct((8, rows), jnp.float32),
        ),
        in_specs=[pl.BlockSpec(memory_space=pltpu.SMEM), hbm, hbm, vmem],
        out_specs=(vmem, vmem),
        scratch_shapes=[
            pltpu.VMEM(xall.shape, xall.dtype),
            pltpu.VMEM(wall.shape, wall.dtype),
            pltpu.VMEM((rows, side), jnp.float32),
            pltpu.SemaphoreType.DMA((2, shards)),
        ],
        compiler_params=pltpu.CompilerParams(vmem_limit_bytes=52 * 1024 * 1024),
        name="layer",
    )(ids, xall, wall, bias)


def means_kernel(groups, shards, neurons, x_ref, rows_ref, all_ref, slots, ssem, rsem):
    bi = lax.axis_index("batch")
    mi = lax.axis_index("mp")
    me = bi * shards + mi
    total = groups * shards
    barrier = pltpu.get_barrier_semaphore()

    def peer(d):
        to = (me + d) % total
        return to // shards, to % shards

    @pl.loop(1, total)
    def _(d):
        pl.semaphore_signal(barrier, inc=1, device_id=peer(d), device_id_type=MESH)

    pl.semaphore_wait(barrier, total - 1)

    def copy(d, slot):
        return pltpu.make_async_remote_copy(
            src_ref=x_ref,
            dst_ref=slots.at[slot],
            send_sem=ssem.at[d],
            recv_sem=rsem.at[slot],
            device_id=peer(d),
            device_id_type=MESH,
        )

    @pl.loop(1, total)
    def _(d):
        copy(d, me).start()

    slots[me] = x_ref[...]

    @pl.loop(1, total)
    def _(d):
        copy(d, (me + d) % total).wait_recv()

    whole = jnp.zeros(all_ref.shape, jnp.float32)
    for b in range(groups):
        one = slots[b * shards]
        for m in range(1, shards):
            one = one + slots[b * shards + m]
        whole = whole + one / neurons
    all_ref[...] = whole
    mine = slots[bi * shards]
    for m in range(1, shards):
        mine = mine + slots[bi * shards + m]
    rows_ref[...] = mine / neurons

    @pl.loop(1, total)
    def _(d):
        copy(d, me).wait_send()


def means(groups, shards, neurons, sums):
    total = groups * shards
    if total > 64:
        shard_sum = lax.psum(sums[0], "mp") / neurons
        return shard_sum, lax.psum(shard_sum, "batch")
    vmem = pl.BlockSpec(memory_space=pltpu.VMEM)
    like = jax.ShapeDtypeStruct(sums.shape, jnp.float32)
    mine, whole = pl.pallas_call(
        functools.partial(means_kernel, groups, shards, neurons),
        out_shape=(like, like),
        in_specs=[vmem],
        out_specs=(vmem, vmem),
        scratch_shapes=[
            pltpu.VMEM((total,) + sums.shape, jnp.float32),
            pltpu.SemaphoreType.DMA((total,)),
            pltpu.SemaphoreType.DMA((total,)),
        ],
        compiler_params=pltpu.CompilerParams(collective_id=20, has_side_effects=True),
        name="means",
    )(sums)
    return mine[0], whole[0]


def on_device(geo, features, tiles, biases, in_block):
    shards = lax.axis_size("mp")
    groups = lax.axis_size("batch")
    me = lax.axis_index("mp")
    rows = features.shape[0]
    side = tiles.shape[4]
    cb = tiles.shape[1]
    fan = tiles.shape[2]
    current = features
    mine = lax.dynamic_slice_in_dim(in_block, me * cb, cb, axis=1) % cb
    for layer in range(tiles.shape[0]):
        wall, xall = gather(geo, shards, groups, layer, tiles, current)
        current, sums = apply_layer(
            mine[layer].reshape(-1), xall, wall, biases[layer].reshape(1, -1)
        )
    row_means, whole = means(groups, shards, cb * side * shards, sums)
    grand = jnp.sum(whole) / (rows * groups)
    return (current, row_means, grand)


def solution(mesh):
    placed = (P("batch", "mp"), P(None, "mp", None, "batch", None), P(None, "mp"), P())
    return jax.shard_map(
        functools.partial(on_device, geometry(mesh)),
        mesh=mesh,
        in_specs=placed,
        out_specs=(P("batch", "mp"), P("batch"), P()),
        check_vma=False,
    )
```

profile of v0, /device:TPU:0, one launch (start us, length us, event | category | flops | bytes accessed | tf_op | source)
XLA Modules:
  0.0 307.4 jit_solution(18066144932089241264)
XLA Ops:
  0.6 0.7 and_select_fusion
  1.3 0.1 copy.8
  1.5 0.2 reshape_squeeze.7.ids
  1.7 132.8 %gather_0.1 = (bf16[8,128,3,16,128]{4,3,2,1,0:T(8,128)(2,1)}, bf16[4,128,16384]{2,1,0:T(8,128)(2,1)}) custom-call(bf16[2,128,3,16,128]{4,3,2,1,0:T(8,128)(2,1)} %tiles.3, bf16[128,16384]{1,0:T(8,128)(2,1)} %cur.1), custom_call_target="tpu_custom_call" | custom-call | tf_op jit(solution)/shard_map/gather_0/pallas_call | solution.py:230
  134.4 1.1 fusion.1
  135.5 13.8 %layer.2 = (bf16[128,16384]{1,0:T(8,128)(2,1)}, f32[8,128]{1,0:T(8,128)}) custom-call(s32[384]{0:T(512)S(1)} %reshape_squeeze.7.ids, bf16[4,128,16384]{2,1,0:T(8,128)(2,1)} %get-tuple-element.12.x_ref, bf16[8,128,3,16,128]{4,3,2,1,0:T(8,128)(2,1)} %get-tuple-element.13.w_ref, f32[1,16384]{1,0:T(1,128)S(1)} %get-tuple-element.22.b_ref), custom_call_target="tpu_custom_call" | custom-call | tf_op jit(solution)/shard_map/layer/pallas_call | solution.py:308
  149.4 129.2 %gather_1.1 = (bf16[8,128,3,16,128]{4,3,2,1,0:T(8,128)(2,1)}, bf16[4,128,16384]{2,1,0:T(8,128)(2,1)}) custom-call(bf16[2,128,3,16,128]{4,3,2,1,0:T(8,128)(2,1)} %tiles.3, bf16[128,16384]{1,0:T(8,128)(2,1)} %get-tuple-element.14.cur), custom_call_target="tpu_custom_call" | custom-call | tf_op jit(solution)/shard_map/gather_1/pallas_call | solution.py:230
  278.6 0.1 copy.7
  278.7 0.2 reshape_squeeze.6.ids
  278.9 13.8 %layer.3 = (bf16[128,16384]{1,0:T(8,128)(2,1)}, f32[8,128]{1,0:T(8,128)S(1)}) custom-call(s32[384]{0:T(512)S(1)} %reshape_squeeze.6.ids, bf16[4,128,16384]{2,1,0:T(8,128)(2,1)} %get-tuple-element.15.x_ref, bf16[8,128,3,16,128]{4,3,2,1,0:T(8,128)(2,1)} %get-tuple-element.16.w_ref, f32[1,16384]{1,0:T(1,128)S(1)} %get-tuple-element.21.b_ref), custom_call_target="tpu_custom_call" | custom-call | tf_op jit(solution)/shard_map/layer/pallas_call | solution.py:308
  292.8 0.0 copy-start
  292.8 0.6 copy-done
  293.4 9.7 %means.1 = (f32[8,128]{1,0:T(8,128)}, f32[8,128]{1,0:T(8,128)}) custom-call(f32[8,128]{1,0:T(8,128)} %copy-done), custom_call_target="tpu_custom_call" | custom-call | tf_op jit(solution)/shard_map/means/pallas_call | solution.py:388
  303.1 1.3 slice_reduce_fusion
  305.0 1.2 slice_bitcast_fusion
  (1 shorter events, 0.0 us)
Async XLA Ops:
  292.8 0.6 copy-start
where the time goes:
time: 308 us; the launch traced here: 307 us
  Pallas kernels  299 us (97%)
  local copies, waits for them, and re-layouts  3.52 us (1%)
    pallas_call x2, Pallas kernels, gather(): pl.pallas_call(functools.partial(gather_kernel, geo, shards, layer, piece...  262 us
    pallas_call x2, Pallas kernels, apply_layer(): pl.pallas_call(layer_kernel, out_shape=(jax.ShapeDtypeStruct((rows, width...  27.7 us
    pallas_call x1, Pallas kernels, means(): pl.pallas_call(functools.partial(means_kernel, groups, shards, neurons),...  9.72 us

commit v1 on v0

--- a/solution.py
+++ b/solution.py
@@ -9,6 +9,7 @@
 from jax.sharding import PartitionSpec as P
 
 MESH = pl.DeviceIdType.MESH
+PIECES = 4
 
 
 def geometry(mesh):
@@ -401,6 +402,443 @@
     return mine[0], whole[0]
 
 
+def fused_kernel(
+    geo, pieces, neurons, total_rows,
+    ids, feats, tiles, biases, out, rows_ref, grand_ref,
+    wl, bl, xin, x2, st, fin, sums, line, slots,
+    lsem, qsend, qrecv, bsend, brecv, up, dn, xs, wrecv,
+    osend, orecv, msend, mrecv,
+):
+    nl, nq, line_major, nc = geo
+    layers, groups, shards, per, fan, _, side = wl.shape
+    ny = shards // nc
+    cb = per * shards
+    n = per // pieces
+    chunks = shards * pieces
+    every = layers * chunks
+    depth = nl
+    bi = lax.axis_index("batch")
+    mi = lax.axis_index("mp")
+    if line_major:
+        l, q = bi // nq, bi % nq
+    else:
+        l, q = bi % nl, bi // nl
+    y, core = mi // nc, mi % nc
+    side_q = (q + 1) % nq
+    total = groups * shards
+    me = bi * shards + mi
+
+    def group(level, column):
+        return level * nq + column if line_major else column * nl + level
+
+    def source(k):
+        return ((y + k // nc) % ny) * nc + (core + k % nc) % nc
+
+    def spot(p):
+        c = p % chunks
+        return p // chunks, c // pieces, c % pieces
+
+    def peer(d):
+        to = (me + d) % total
+        return to // shards, to % shards
+
+    @pl.loop(0, cb)
+    def _(j):
+        pltpu.make_async_copy(
+            feats.at[:, pl.ds(j * side, side)], xin.at[j], lsem.at[0]
+        ).start()
+
+    def own_quarter(layer):
+        return pltpu.make_async_copy(
+            tiles.at[layer, pl.ds(mi * per, per)], wl.at[layer, bi, mi], lsem.at[2 + layer]
+        )
+
+    for layer in range(layers):
+        own_quarter(layer).start()
+    mine_b = pl.ds(mi * per * side, per * side)
+    in_b = pltpu.make_async_copy(biases.at[:, mine_b], bl.at[:, mine_b], lsem.at[1])
+    in_b.start()
+
+    barrier = pltpu.get_barrier_semaphore()
+
+    @pl.loop(1, total)
+    def _(d):
+        pl.semaphore_signal(barrier, inc=1, device_id=peer(d), device_id_type=MESH)
+
+    pl.semaphore_wait(barrier, total - 1)
+
+    def quarter(layer, k):
+        to = source(k)
+        return pltpu.make_async_remote_copy(
+            src_ref=tiles.at[layer, pl.ds(to * per, per)],
+            dst_ref=wl.at[layer, bi, mi],
+            send_sem=qsend.at[layer, k],
+            recv_sem=qrecv.at[layer, mi],
+            device_id=(bi, to),
+            device_id_type=MESH,
+        )
+
+    def quarter_in(layer, k):
+        m = source(k)
+        return pltpu.make_async_remote_copy(
+            src_ref=wl.at[layer, bi, m],
+            dst_ref=wl.at[layer, bi, m],
+            send_sem=qsend.at[layer, 0],
+            recv_sem=qrecv.at[layer, m],
+            device_id=(bi, m),
+            device_id_type=MESH,
+        )
+
+    def bias_out(k):
+        to = source(k)
+        return pltpu.make_async_remote_copy(
+            src_ref=biases.at[:, pl.ds(to * per * side, per * side)],
+            dst_ref=bl.at[:, mine_b],
+            send_sem=bsend.at[k],
+            recv_sem=brecv.at[mi],
+            device_id=(bi, to),
+            device_id_type=MESH,
+        )
+
+    def bias_in(k):
+        m = source(k)
+        part = bl.at[:, pl.ds(m * per * side, per * side)]
+        return pltpu.make_async_remote_copy(
+            src_ref=part, dst_ref=part, send_sem=bsend.at[0], recv_sem=brecv.at[m],
+            device_id=(bi, m), device_id_type=MESH,
+        )
+
+    for k in range(1, shards):
+        quarter(0, k).start()
+        bias_out(k).start()
+    for layer in range(1, layers):
+        for k in range(1, shards):
+            quarter(layer, k).start()
+    sums[...] = jnp.zeros_like(sums)
+
+    def wcopy(p, b, to, ssem):
+        layer, k, g = spot(p)
+        part = wl.at[layer, b, source(k), pl.ds(g * n, n)]
+        return pltpu.make_async_remote_copy(
+            src_ref=part,
+            dst_ref=part,
+            send_sem=ssem,
+            recv_sem=wrecv.at[b, p],
+            device_id=(to, mi),
+            device_id_type=MESH,
+        )
+
+    def relay(p, level, to):
+        return (p % 2 == 1) & ((level // 2) == (to // 2)) & (level != to)
+
+    def flow(t, drain):
+        def go(cond, copy):
+            @pl.when(cond)
+            def _():
+                copy.wait_send() if drain else copy.start()
+
+        def arrive(p, b):
+            if not drain:
+                wcopy(p, b, bi, up.at[0, p]).wait_recv()
+
+        def raise_(p, b, e):
+            go(l < nl - 1, wcopy(p, b, group(jnp.minimum(l + 1, nl - 1), q), up.at[e, p]))
+
+        def lower(p, b, e):
+            go(l > 0, wcopy(p, b, group(jnp.maximum(l - 1, 0), q), dn.at[e, p]))
+
+        def cross(p, b, level, cond):
+            go(cond, wcopy(p, b, group(l, side_q), xs.at[level, p]))
+
+        @pl.when(t < every)
+        def _():
+            if not drain:
+                layer, k, g = spot(t)
+
+                @pl.when((g == 0) & (k == 0))
+                def _():
+                    pltpu.make_async_copy(
+                        tiles.at[layer, pl.ds(mi * per, per)],
+                        wl.at[layer, bi, mi],
+                        lsem.at[2 + layer],
+                    ).wait()
+
+                @pl.when((g == 0) & (k > 0))
+                def _():
+                    quarter_in(layer, k).wait_recv()
+
+            raise_(t, bi, 0)
+            lower(t, bi, 0)
+            cross(t, bi, l, True)
+
+        for d in range(1, nl):
+            p = t - d
+
+            @pl.when((p >= 0) & (p < every))
+            def _(d=d, p=p):
+                @pl.when(l - d >= 0)
+                def _():
+                    b = group(jnp.maximum(l - d, 0), q)
+                    arrive(p, b)
+                    raise_(p, b, d)
+                    cross(p, b, jnp.maximum(l - d, 0), jnp.logical_not(relay(p, l - d, l)))
+
+                @pl.when(l + d <= nl - 1)
+                def _():
+                    b = group(jnp.minimum(l + d, nl - 1), q)
+                    arrive(p, b)
+                    lower(p, b, d)
+                    cross(p, b, jnp.minimum(l + d, nl - 1), jnp.logical_not(relay(p, l + d, l)))
+
+                if d == 1:
+                    @pl.when(p % 2 == 1)
+                    def _():
+                        b = group(l, side_q)
+                        arrive(p, b)
+                        go(l % 2 == 0, wcopy(p, b, group(jnp.minimum(l + 1, nl - 1), q), up.at[nl, p]))
+                        go(l % 2 == 1, wcopy(p, b, group(jnp.maximum(l - 1, 0), q), dn.at[nl, p]))
+
+    def landing(p):
+        for level in range(nl):
+            b = group(level, side_q)
+
+            @pl.when((level != l) | (p % 2 == 0))
+            def _(b=b):
+                wcopy(p, b, bi, up.at[0, p]).wait_recv()
+
+    def kept(layer, k, g):
+        if layer < layers - 1:
+            return st.at[k, pl.ds(g * n, n)]
+        return fin.at[k, :, pl.ds(g * n * side, n * side)]
+
+    def place(layer, m, g):
+        if layer < layers - 1:
+            return x2.at[pl.ds(m * per + g * n, n)]
+        return out.at[:, pl.ds((m * per + g * n) * side, n * side)]
+
+    def ocopy(layer, c):
+        k, g = c // pieces, c % pieces
+        return pltpu.make_async_remote_copy(
+            src_ref=kept(layer, k, g),
+            dst_ref=place(layer, mi, g),
+            send_sem=osend.at[layer, c],
+            recv_sem=orecv.at[layer, mi, g],
+            device_id=(bi, source(k)),
+            device_id_type=MESH,
+        )
+
+    def okeep(layer, g):
+        return pltpu.make_async_copy(
+            kept(layer, 0, g), place(layer, mi, g), osend.at[layer, g]
+        )
+
+    def ocopy_in(layer, m, g):
+        part = place(layer, m, g)
+        return pltpu.make_async_remote_copy(
+            src_ref=part, dst_ref=part, send_sem=osend.at[layer, g],
+            recv_sem=orecv.at[layer, m, g], device_id=(bi, m), device_id_type=MESH,
+        )
+
+    def hand_on(p):
+        for layer in range(layers):
+            c = p - layer * chunks
+
+            @pl.when((c >= 0) & (c < pieces))
+            def _(layer=layer, c=c):
+                okeep(layer, c).start()
+
+            @pl.when((c >= pieces) & (c < chunks))
+            def _(layer=layer, c=c):
+                ocopy(layer, c).start()
+
+    def results_in(layer):
+        @pl.loop(0, pieces)
+        def _(g):
+            okeep(layer, g).wait()
+            for k in range(1, shards):
+                ocopy_in(layer, source(k), g).wait_recv()
+
+    def compute(layer, c):
+        k, g = c // pieces, c % pieces
+        m = source(k)
+        src = xin if layer == 0 else x2
+        for jj in range(n):
+            j = g * n + jj
+            base = ((layer * shards + m) * cb + mi * per + j) * fan
+            xparts, wparts = [], []
+            for t in range(fan):
+                at = ids[base + t]
+                xparts.append(src[at])
+                wparts.append(wl[layer, :, m, j, t].reshape(side, side))
+            whole = jnp.dot(
+                jnp.concatenate(xparts, axis=1),
+                jnp.concatenate(wparts, axis=0),
+                preferred_element_type=jnp.float32,
+            )
+            bias = bl[layer : layer + 1, pl.ds(pl.multiple_of((m * per + j) * side, side), side)]
+            res = jnp.clip(whole + bias, 0.0, 32.0).astype(out.dtype)
+            if layer < layers - 1:
+                st[k, j] = res
+            else:
+                fin[k, :, pl.ds(pl.multiple_of(j * side, side), side)] = res
+                sums[...] += res.astype(jnp.float32)
+
+    @pl.loop(0, every + depth + 1)
+    def _(t):
+        flow(t, False)
+        p = t - depth
+
+        @pl.when(p >= 1)
+        def _():
+            hand_on(p - 1)
+
+        @pl.when(p == 0)
+        def _():
+            pltpu.make_async_copy(xin, xin, lsem.at[0]).wait()
+            in_b.wait()
+            for k in range(1, shards):
+                bias_in(k).wait_recv()
+
+        for layer in range(layers):
+            if layer > 0:
+                @pl.when(p == layer * chunks)
+                def _(layer=layer):
+                    results_in(layer - 1)
+
+            @pl.when((p >= layer * chunks) & (p < (layer + 1) * chunks))
+            def _(layer=layer):
+                landing(p)
+                compute(layer, p - layer * chunks)
+
+    line[...] = jnp.broadcast_to(jnp.sum(sums[...].T, axis=0, keepdims=True), line.shape)
+
+    @pl.loop(0, every + depth)
+    def _(t):
+        flow(t, True)
+
+    for layer in range(layers):
+        for k in range(1, shards):
+            quarter(layer, k).wait_send()
+    for k in range(1, shards):
+        bias_out(k).wait_send()
+
+    def mcopy(d, slot):
+        return pltpu.make_async_remote_copy(
+            src_ref=line,
+            dst_ref=slots.at[slot],
+            send_sem=msend.at[d],
+            recv_sem=mrecv.at[slot],
+            device_id=peer(d),
+            device_id_type=MESH,
+        )
+
+    @pl.loop(1, total)
+    def _(d):
+        mcopy(d, me).start()
+
+    slots[me] = line[...]
+    for layer in range(layers):
+        @pl.loop(pieces, chunks)
+        def _(c, layer=layer):
+            ocopy(layer, c).wait_send()
+
+    @pl.loop(1, total)
+    def _(d):
+        mcopy(d, (me + d) % total).wait_recv()
+
+    whole = jnp.zeros(line.shape, jnp.float32)
+    for b in range(groups):
+        one = slots[b * shards]
+        for m in range(1, shards):
+            one = one + slots[b * shards + m]
+        whole = whole + one / neurons
+    mine = slots[bi * shards]
+    for m in range(1, shards):
+        mine = mine + slots[bi * shards + m]
+    rows_ref[...] = mine / neurons
+    grand_ref[0, 0] = jnp.sum(whole[0:1]) / total_rows
+    results_in(layers - 1)
+
+    @pl.loop(1, total)
+    def _(d):
+        mcopy(d, me).wait_send()
+
+
+def fused(geo, pieces, features, tiles, biases, in_block):
+    nl, nq, _, nc = geo
+    shards = lax.axis_size("mp")
+    groups = lax.axis_size("batch")
+    layers, cb, fan, depth, side = tiles.shape
+    rows, width = features.shape
+    per = cb // shards
+    chunks = shards * pieces
+    every = layers * chunks
+    total = groups * shards
+    dma = pltpu.SemaphoreType.DMA
+    hbm = pl.BlockSpec(memory_space=pl.ANY)
+    acts, row_means, grand = pl.pallas_call(
+        functools.partial(
+            fused_kernel, geo, pieces, cb * side * shards, rows * groups
+        ),
+        out_shape=(
+            jax.ShapeDtypeStruct((rows, width), features.dtype),
+            jax.ShapeDtypeStruct((8, rows), jnp.float32),
+            jax.ShapeDtypeStruct((1, 1), jnp.float32),
+        ),
+        in_specs=[pl.BlockSpec(memory_space=pltpu.SMEM), hbm, hbm, hbm],
+        out_specs=(
+            hbm,
+            pl.BlockSpec(memory_space=pltpu.VMEM),
+            pl.BlockSpec(memory_space=pltpu.SMEM),
+        ),
+        scratch_shapes=[
+            pltpu.VMEM((layers, groups, shards, per, fan, depth, side), tiles.dtype),
+            pltpu.VMEM(biases.shape, biases.dtype),
+            pltpu.VMEM((cb, rows, side), features.dtype),
+            pltpu.VMEM((cb, rows, side), features.dtype),
+            pltpu.VMEM((shards, per, rows, side), features.dtype),
+            pltpu.VMEM((shards, rows, per * side), features.dtype),
+            pltpu.VMEM((rows, side), jnp.float32),
+            pltpu.VMEM((8, rows), jnp.float32),
+            pltpu.VMEM((total, 8, rows), jnp.float32),
+            dma((2 + layers,)),
+            dma((layers, shards)),
+            dma((layers, shards)),
+            dma((shards,)),
+            dma((shards,)),
+            dma((nl + 1, every)),
+            dma((nl + 1, every)),
+            dma((nl, every)),
+            dma((groups, every)),
+            dma((layers, chunks)),
+            dma((layers, shards, pieces)),
+            dma((total,)),
+            dma((total,)),
+        ],
+        compiler_params=pltpu.CompilerParams(
+            collective_id=3,
+            has_side_effects=True,
+            vmem_limit_bytes=62 * 1024 * 1024,
+        ),
+        name="net",
+    )((in_block % cb).reshape(-1), features, tiles, biases)
+    return acts, row_means[0], grand[0, 0]
+
+
+def suits(geo, shards, groups, features, tiles, biases):
+    nl, nq, _, _ = geo
+    kept = 2 * features.size + 2 * features.size + groups * tiles.size
+    return (
+        nq == 2
+        and nl % 2 == 0
+        and tiles.shape[0] == 2
+        and tiles.shape[3] % 16 == 0
+        and tiles.shape[1] // shards % PIECES == 0
+        and groups * shards <= 64
+        and 2 * kept < 56 * 1024 * 1024
+    )
+
+
 def on_device(geo, features, tiles, biases, in_block):
     shards = lax.axis_size("mp")
     groups = lax.axis_size("batch")
@@ -409,6 +847,8 @@
     side = tiles.shape[4]
     cb = tiles.shape[1]
     fan = tiles.shape[2]
+    if suits(geo, shards, groups, features, tiles, biases):
+        return fused(geo, PIECES, features, tiles, biases, in_block)
     current = features
     mine = lax.dynamic_slice_in_dim(in_block, me * cb, cb, axis=1) % cb
     for layer in range(tiles.shape[0]):

time: 308 us -> 288 us (0.935)
  Pallas kernels: 299 us -> 278 us
  local copies, waits for them, and re-layouts: 3.52 us -> 6.86 us
    pallas_call x5 -> x1, Pallas kernels: 299 us -> 278 us  [fused(): pl.pallas_call(functools.partial(fused_kernel, geo, pieces, cb * side * s...]
    unnamed x2 -> x1, local copies, waits for them, and re-layouts: 0.59 us -> 4.57 us
where the time goes in v1:
time: 288 us
  Pallas kernels  278 us (97%)
  local copies, waits for them, and re-layouts  6.86 us (2%)
    pallas_call x1, Pallas kernels, fused(): pl.pallas_call(functools.partial(fused_kernel, geo, pieces, cb * side * s...  278 us

profile of v1, /device:TPU:0, one launch (start us, length us, event | category | flops | bytes accessed | tf_op | source)
XLA Modules:
  0.0 288.1 jit_solution(14478485931026114894)
XLA Ops:
  0.6 0.7 and_select_fusion
  1.4 0.2 copy.7
  1.6 0.9 reshape.9.ids
  2.5 278.0 %net.1 = (bf16[128,16384]{1,0:T(8,128)(2,1)}, f32[8,128]{1,0:T(8,128)}, f32[1,1]{1,0:T(1,128)}) custom-call(s32[3072]{0:T(1024)} %reshape.9.ids, bf16[128,16384]{1,0:T(8,128)(2,1)} %feats.1, bf16[2,128,3,16,128]{4,3,2,1,0:T(8,128)(2,1)} %tiles.1, f32[2,16384]{1,0:T(2,128)} %biases.1), custom_call_target="tpu_custom_call" | custom-call | tf_op jit(solution)/shard_map/net/pallas_call | solution.py:779
  280.5 1.2 slice_bitcast_fusion
  281.7 4.6 %copy.10 = bf16[128,16384]{1,0:T(8,128)(2,1)} copy(bf16[128,16384]{1,0:T(8,128)(2,1)} %get-tuple-element.12) | data formatting | bytes 8388608

commit v2 on v1

--- a/solution.py
+++ b/solution.py
@@ -10,6 +10,7 @@
 
 MESH = pl.DeviceIdType.MESH
 PIECES = 4
+HOP = 1
 
 
 def geometry(mesh):
@@ -406,8 +407,8 @@
     geo, pieces, neurons, total_rows,
     ids, feats, tiles, biases, out, rows_ref, grand_ref,
     wl, bl, xin, x2, st, fin, sums, line, slots,
-    lsem, qsend, qrecv, bsend, brecv, up, dn, xs, wrecv,
-    osend, orecv, msend, mrecv,
+    lsem, qsend, qrecv, bsem, up, dn, xs, wrecv, xrecv, rrecv,
+    osend, okept, orecv, msem,
 ):
     nl, nq, line_major, nc = geo
     layers, groups, shards, per, fan, _, side = wl.shape
@@ -416,7 +417,8 @@
     n = per // pieces
     chunks = shards * pieces
     every = layers * chunks
-    depth = nl
+    depth = HOP * nl
+    half = every
     bi = lax.axis_index("batch")
     mi = lax.axis_index("mp")
     if line_major:
@@ -434,9 +436,13 @@
     def source(k):
         return ((y + k // nc) % ny) * nc + (core + k % nc) % nc
 
+    def turn(layer, c):
+        k = c // pieces
+        return jnp.where(layer == layers - 1, shards - 1 - k, k) if layers > 1 else k
+
     def spot(p):
         c = p % chunks
-        return p // chunks, c // pieces, c % pieces
+        return p // chunks, turn(p // chunks, c), c % pieces
 
     def peer(d):
         to = (me + d) % total
@@ -461,18 +467,29 @@
 
     barrier = pltpu.get_barrier_semaphore()
 
-    @pl.loop(1, total)
-    def _(d):
-        pl.semaphore_signal(barrier, inc=1, device_id=peer(d), device_id_type=MESH)
-
-    pl.semaphore_wait(barrier, total - 1)
+    def greet(b, m):
+        pl.semaphore_signal(barrier, inc=1, device_id=(b, m), device_id_type=MESH)
+
+    @pl.when(l > 0)
+    def _():
+        greet(group(l - 1, q), mi)
+
+    @pl.when(l < nl - 1)
+    def _():
+        greet(group(l + 1, q), mi)
+
+    greet(group(l, side_q), mi)
+    for k in range(1, shards):
+        greet(bi, source(k))
+    near = jnp.where(l > 0, 1, 0) + jnp.where(l < nl - 1, 1, 0)
+    pl.semaphore_wait(barrier, near + shards)
 
     def quarter(layer, k):
         to = source(k)
         return pltpu.make_async_remote_copy(
             src_ref=tiles.at[layer, pl.ds(to * per, per)],
             dst_ref=wl.at[layer, bi, mi],
-            send_sem=qsend.at[layer, k],
+            send_sem=qsend,
             recv_sem=qrecv.at[layer, mi],
             device_id=(bi, to),
             device_id_type=MESH,
@@ -483,7 +500,7 @@
         return pltpu.make_async_remote_copy(
             src_ref=wl.at[layer, bi, m],
             dst_ref=wl.at[layer, bi, m],
-            send_sem=qsend.at[layer, 0],
+            send_sem=qsend,
             recv_sem=qrecv.at[layer, m],
             device_id=(bi, m),
             device_id_type=MESH,
@@ -494,18 +511,17 @@
         return pltpu.make_async_remote_copy(
             src_ref=biases.at[:, pl.ds(to * per * side, per * side)],
             dst_ref=bl.at[:, mine_b],
-            send_sem=bsend.at[k],
-            recv_sem=brecv.at[mi],
+            send_sem=bsem.at[0],
+            recv_sem=bsem.at[1],
             device_id=(bi, to),
             device_id_type=MESH,
         )
 
-    def bias_in(k):
-        m = source(k)
-        part = bl.at[:, pl.ds(m * per * side, per * side)]
+    def biases_of_others():
+        part = bl.at[:, pl.ds(0, (shards - 1) * per * side)]
         return pltpu.make_async_remote_copy(
-            src_ref=part, dst_ref=part, send_sem=bsend.at[0], recv_sem=brecv.at[m],
-            device_id=(bi, m), device_id_type=MESH,
+            src_ref=part, dst_ref=part, send_sem=bsem.at[0], recv_sem=bsem.at[1],
+            device_id=(bi, mi), device_id_type=MESH,
         )
 
     for k in range(1, shards):
@@ -516,95 +532,142 @@
             quarter(layer, k).start()
     sums[...] = jnp.zeros_like(sums)
 
-    def wcopy(p, b, to, ssem):
+    def wcopy(p, b, to, ssem, rsem):
         layer, k, g = spot(p)
         part = wl.at[layer, b, source(k), pl.ds(g * n, n)]
         return pltpu.make_async_remote_copy(
             src_ref=part,
             dst_ref=part,
             send_sem=ssem,
-            recv_sem=wrecv.at[b, p],
+            recv_sem=rsem,
             device_id=(to, mi),
             device_id_type=MESH,
         )
 
+    def sent(part, ssem):
+        pltpu.make_async_remote_copy(
+            src_ref=part, dst_ref=part, send_sem=ssem, recv_sem=rrecv.at[0],
+            device_id=(bi, mi), device_id_type=MESH,
+        ).wait_send()
+
     def relay(p, level, to):
         return (p % 2 == 1) & ((level // 2) == (to // 2)) & (level != to)
 
-    def flow(t, drain):
+    def flow(t):
         def go(cond, copy):
             @pl.when(cond)
             def _():
-                copy.wait_send() if drain else copy.start()
-
-        def arrive(p, b):
-            if not drain:
-                wcopy(p, b, bi, up.at[0, p]).wait_recv()
-
-        def raise_(p, b, e):
-            go(l < nl - 1, wcopy(p, b, group(jnp.minimum(l + 1, nl - 1), q), up.at[e, p]))
-
-        def lower(p, b, e):
-            go(l > 0, wcopy(p, b, group(jnp.maximum(l - 1, 0), q), dn.at[e, p]))
-
-        def cross(p, b, level, cond):
-            go(cond, wcopy(p, b, group(l, side_q), xs.at[level, p]))
+                copy.start()
+
+        def arrive(p, level):
+            wcopy(p, bi, bi, up.at[0], wrecv.at[level, p]).wait_recv()
+
+        def raise_(p, b, level, e):
+            to = group(jnp.minimum(l + 1, nl - 1), q)
+            go(l < nl - 1, wcopy(p, b, to, up.at[e], wrecv.at[level, p]))
+
+        def lower(p, b, level, e):
+            to = group(jnp.maximum(l - 1, 0), q)
+            go(l > 0, wcopy(p, b, to, dn.at[e], wrecv.at[level, p]))
+
+        def cross(p, b, level, own):
+            to = group(l, side_q)
+            if own:
+                go(p % 2 == 0, wcopy(p, b, to, xs.at[level], xrecv.at[p]))
+                go(p % 2 == 1, wcopy(p, b, to, xs.at[level], rrecv.at[p]))
+            else:
+                cond = jnp.logical_not(relay(p, level, l))
+                go(cond, wcopy(p, b, to, xs.at[level], xrecv.at[p]))
+
+        def at(early, late):
+            first, second = t - HOP * early, t - HOP * late
+            p = jnp.where(first < half, first, second)
+            return p, (p >= 0) & (p < every) & ((first < half) | (second >= half))
+
+        below, above = l, nl - 1 - l
+        turn_x = jnp.maximum(below, above) - 1
 
         @pl.when(t < every)
         def _():
-            if not drain:
-                layer, k, g = spot(t)
-
-                @pl.when((g == 0) & (k == 0))
-                def _():
-                    pltpu.make_async_copy(
-                        tiles.at[layer, pl.ds(mi * per, per)],
-                        wl.at[layer, bi, mi],
-                        lsem.at[2 + layer],
-                    ).wait()
-
-                @pl.when((g == 0) & (k > 0))
-                def _():
-                    quarter_in(layer, k).wait_recv()
-
-            raise_(t, bi, 0)
-            lower(t, bi, 0)
-            cross(t, bi, l, True)
+            layer, k, g = spot(t)
+
+            @pl.when((g == 0) & (k == 0))
+            def _():
+                own_quarter(layer).wait()
+
+            @pl.when((g == 0) & (k > 0))
+            def _():
+                quarter_in(layer, k).wait_recv()
+
+        p, ok = at(0, below)
+
+        @pl.when(ok)
+        def _(p=p):
+            raise_(p, bi, l, 0)
+
+        p, ok = at(0, above)
+
+        @pl.when(ok)
+        def _(p=p):
+            lower(p, bi, l, 0)
+
+        p, ok = at(0, turn_x)
+
+        @pl.when(ok)
+        def _(p=p):
+            cross(p, bi, l, True)
+
+        def across(p):
+            b = group(l, side_q)
+            wcopy(p, b, bi, up.at[0], rrecv.at[p]).wait_recv()
+            upper = group(jnp.minimum(l + 1, nl - 1), q)
+            under = group(jnp.maximum(l - 1, 0), q)
+            go(l % 2 == 0, wcopy(p, b, upper, up.at[nl], xrecv.at[p]))
+            go(l % 2 == 1, wcopy(p, b, under, dn.at[nl], xrecv.at[p]))
 
         for d in range(1, nl):
-            p = t - d
-
-            @pl.when((p >= 0) & (p < every))
+            p, ok = at(d, below)
+
+            @pl.when(ok & (l - d >= 0))
             def _(d=d, p=p):
-                @pl.when(l - d >= 0)
-                def _():
-                    b = group(jnp.maximum(l - d, 0), q)
-                    arrive(p, b)
-                    raise_(p, b, d)
-                    cross(p, b, jnp.maximum(l - d, 0), jnp.logical_not(relay(p, l - d, l)))
-
-                @pl.when(l + d <= nl - 1)
-                def _():
-                    b = group(jnp.minimum(l + d, nl - 1), q)
-                    arrive(p, b)
-                    lower(p, b, d)
-                    cross(p, b, jnp.minimum(l + d, nl - 1), jnp.logical_not(relay(p, l + d, l)))
-
-                if d == 1:
-                    @pl.when(p % 2 == 1)
-                    def _():
-                        b = group(l, side_q)
-                        arrive(p, b)
-                        go(l % 2 == 0, wcopy(p, b, group(jnp.minimum(l + 1, nl - 1), q), up.at[nl, p]))
-                        go(l % 2 == 1, wcopy(p, b, group(jnp.maximum(l - 1, 0), q), dn.at[nl, p]))
+                level = jnp.maximum(l - d, 0)
+                arrive(p, level)
+                raise_(p, group(level, q), level, d)
+                cross(p, group(level, q), level, False)
+
+            p, ok = at(d, above)
+
+            @pl.when(ok & (l + d <= nl - 1))
+            def _(d=d, p=p):
+                level = jnp.minimum(l + d, nl - 1)
+                arrive(p, level)
+                lower(p, group(level, q), level, d)
+                cross(p, group(level, q), level, False)
+
+            if d == 1:
+                p, ok = at(1, turn_x + 1)
+
+                @pl.when(ok & (p % 2 == 1))
+                def _(p=p):
+                    across(p)
 
     def landing(p):
-        for level in range(nl):
-            b = group(level, side_q)
-
-            @pl.when((level != l) | (p % 2 == 0))
-            def _(b=b):
-                wcopy(p, b, bi, up.at[0, p]).wait_recv()
+        layer, k, g = spot(p)
+
+        def wait(count):
+            part = wl.at[layer, pl.ds(0, count), source(k), pl.ds(g * n, n)]
+            pltpu.make_async_remote_copy(
+                src_ref=part, dst_ref=part, send_sem=up.at[0], recv_sem=xrecv.at[p],
+                device_id=(bi, mi), device_id_type=MESH,
+            ).wait_recv()
+
+        @pl.when(p % 2 == 0)
+        def _():
+            wait(nl)
+
+        @pl.when(p % 2 == 1)
+        def _():
+            wait(nl - 1)
 
     def kept(layer, k, g):
         if layer < layers - 1:
@@ -617,57 +680,60 @@
         return out.at[:, pl.ds((m * per + g * n) * side, n * side)]
 
     def ocopy(layer, c):
-        k, g = c // pieces, c % pieces
+        k, g = turn(layer, c), c % pieces
         return pltpu.make_async_remote_copy(
             src_ref=kept(layer, k, g),
             dst_ref=place(layer, mi, g),
-            send_sem=osend.at[layer, c],
-            recv_sem=orecv.at[layer, mi, g],
+            send_sem=osend.at[layer],
+            recv_sem=orecv.at[layer],
             device_id=(bi, source(k)),
             device_id_type=MESH,
         )
 
     def okeep(layer, g):
         return pltpu.make_async_copy(
-            kept(layer, 0, g), place(layer, mi, g), osend.at[layer, g]
-        )
-
-    def ocopy_in(layer, m, g):
-        part = place(layer, m, g)
-        return pltpu.make_async_remote_copy(
-            src_ref=part, dst_ref=part, send_sem=osend.at[layer, g],
-            recv_sem=orecv.at[layer, m, g], device_id=(bi, m), device_id_type=MESH,
+            kept(layer, 0, g), place(layer, mi, g), okept.at[layer]
         )
 
     def hand_on(p):
         for layer in range(layers):
             c = p - layer * chunks
 
-            @pl.when((c >= 0) & (c < pieces))
+            inside = (c >= 0) & (c < chunks)
+            k = turn(layer, c)
+
+            @pl.when(inside & (k == 0))
             def _(layer=layer, c=c):
-                okeep(layer, c).start()
-
-            @pl.when((c >= pieces) & (c < chunks))
+                okeep(layer, c % pieces).start()
+
+            @pl.when(inside & (k > 0))
             def _(layer=layer, c=c):
                 ocopy(layer, c).start()
 
+    def others(layer):
+        if layer < layers - 1:
+            return st.at[pl.ds(0, shards - 1)]
+        return fin.at[pl.ds(0, shards - 1)]
+
     def results_in(layer):
-        @pl.loop(0, pieces)
-        def _(g):
-            okeep(layer, g).wait()
-            for k in range(1, shards):
-                ocopy_in(layer, source(k), g).wait_recv()
+        mine = st.at[0] if layer < layers - 1 else fin.at[0]
+        pltpu.make_async_copy(mine, mine, okept.at[layer]).wait()
+        part = others(layer)
+        pltpu.make_async_remote_copy(
+            src_ref=part, dst_ref=part, send_sem=osend.at[layer],
+            recv_sem=orecv.at[layer], device_id=(bi, mi), device_id_type=MESH,
+        ).wait_recv()
 
     def compute(layer, c):
-        k, g = c // pieces, c % pieces
+        k, g = turn(layer, c), c % pieces
         m = source(k)
         src = xin if layer == 0 else x2
         for jj in range(n):
             j = g * n + jj
-            base = ((layer * shards + m) * cb + mi * per + j) * fan
+            column = m * cb + mi * per + j
             xparts, wparts = [], []
             for t in range(fan):
-                at = ids[base + t]
+                at = lax.rem(ids[t, layer, column], cb)
                 xparts.append(src[at])
                 wparts.append(wl[layer, :, m, j, t].reshape(side, side))
             whole = jnp.dot(
@@ -685,7 +751,7 @@
 
     @pl.loop(0, every + depth + 1)
     def _(t):
-        flow(t, False)
+        flow(t)
         p = t - depth
 
         @pl.when(p >= 1)
@@ -696,8 +762,7 @@
         def _():
             pltpu.make_async_copy(xin, xin, lsem.at[0]).wait()
             in_b.wait()
-            for k in range(1, shards):
-                bias_in(k).wait_recv()
+            biases_of_others().wait_recv()
 
         for layer in range(layers):
             if layer > 0:
@@ -712,25 +777,51 @@
 
     line[...] = jnp.broadcast_to(jnp.sum(sums[...].T, axis=0, keepdims=True), line.shape)
 
-    @pl.loop(0, every + depth)
-    def _(t):
-        flow(t, True)
-
-    for layer in range(layers):
-        for k in range(1, shards):
-            quarter(layer, k).wait_send()
-    for k in range(1, shards):
-        bias_out(k).wait_send()
-
     def mcopy(d, slot):
         return pltpu.make_async_remote_copy(
             src_ref=line,
             dst_ref=slots.at[slot],
-            send_sem=msend.at[d],
-            recv_sem=mrecv.at[slot],
+            send_sem=msem.at[0],
+            recv_sem=msem.at[1],
             device_id=peer(d),
             device_id_type=MESH,
         )
+
+    @pl.when(l < nl - 1)
+    def _():
+        for d in range(nl):
+            @pl.when(l - d >= 0)
+            def _(d=d):
+                sent(wl.at[:, bi], up.at[d])
+
+    @pl.when(l > 0)
+    def _():
+        for d in range(nl):
+            @pl.when(l + d <= nl - 1)
+            def _(d=d):
+                sent(wl.at[:, bi], dn.at[d])
+
+    @pl.when(l % 2 == 0)
+    def _():
+        sent(wl.at[0, bi], up.at[nl])
+
+    @pl.when(l % 2 == 1)
+    def _():
+        sent(wl.at[0, bi], dn.at[nl])
+
+    for level in range(nl):
+        paired = (l // 2 == level // 2) & (l != level)
+
+        @pl.when(paired)
+        def _(level=level):
+            sent(wl.at[0, bi], xs.at[level])
+
+        @pl.when(jnp.logical_not(paired))
+        def _(level=level):
+            sent(wl.at[:, bi], xs.at[level])
+
+    sent(wl.at[:, bi, pl.ds(0, shards - 1)], qsend)
+    biases_of_others().wait_send()
 
     @pl.loop(1, total)
     def _(d):
@@ -738,14 +829,13 @@
 
     slots[me] = line[...]
     for layer in range(layers):
-        @pl.loop(pieces, chunks)
-        def _(c, layer=layer):
-            ocopy(layer, c).wait_send()
-
-    @pl.loop(1, total)
-    def _(d):
-        mcopy(d, (me + d) % total).wait_recv()
-
+        sent(others(layer), osend.at[layer])
+    lines = slots.at[pl.ds(0, total - 1)]
+    exchanged = pltpu.make_async_remote_copy(
+        src_ref=lines, dst_ref=lines, send_sem=msem.at[0], recv_sem=msem.at[1],
+        device_id=(bi, mi), device_id_type=MESH,
+    )
+    exchanged.wait_recv()
     whole = jnp.zeros(line.shape, jnp.float32)
     for b in range(groups):
         one = slots[b * shards]
@@ -755,13 +845,10 @@
     mine = slots[bi * shards]
     for m in range(1, shards):
         mine = mine + slots[bi * shards + m]
-    rows_ref[...] = mine / neurons
+    rows_ref[...] = mine[0:1] / neurons
     grand_ref[0, 0] = jnp.sum(whole[0:1]) / total_rows
     results_in(layers - 1)
-
-    @pl.loop(1, total)
-    def _(d):
-        mcopy(d, me).wait_send()
+    exchanged.wait_send()
 
 
 def fused(geo, pieces, features, tiles, biases, in_block):
@@ -775,19 +862,19 @@
     every = layers * chunks
     total = groups * shards
     dma = pltpu.SemaphoreType.DMA
-    hbm = pl.BlockSpec(memory_space=pl.ANY)
+    hbm = pl.BlockSpec(memory_space=pltpu.HBM)
     acts, row_means, grand = pl.pallas_call(
         functools.partial(
             fused_kernel, geo, pieces, cb * side * shards, rows * groups
         ),
         out_shape=(
             jax.ShapeDtypeStruct((rows, width), features.dtype),
-            jax.ShapeDtypeStruct((8, rows), jnp.float32),
+            jax.ShapeDtypeStruct((1, rows), jnp.float32),
             jax.ShapeDtypeStruct((1, 1), jnp.float32),
         ),
         in_specs=[pl.BlockSpec(memory_space=pltpu.SMEM), hbm, hbm, hbm],
         out_specs=(
-            hbm,
+            pl.BlockSpec(memory_space=pl.ANY),
             pl.BlockSpec(memory_space=pltpu.VMEM),
             pl.BlockSpec(memory_space=pltpu.SMEM),
         ),
@@ -802,26 +889,27 @@
             pltpu.VMEM((8, rows), jnp.float32),
             pltpu.VMEM((total, 8, rows), jnp.float32),
             dma((2 + layers,)),
+            dma(()),
             dma((layers, shards)),
-            dma((layers, shards)),
-            dma((shards,)),
-            dma((shards,)),
-            dma((nl + 1, every)),
-            dma((nl + 1, every)),
+            dma((2,)),
+            dma((nl + 1,)),
+            dma((nl + 1,)),
+            dma((nl,)),
             dma((nl, every)),
-            dma((groups, every)),
-            dma((layers, chunks)),
-            dma((layers, shards, pieces)),
-            dma((total,)),
-            dma((total,)),
+            dma((every,)),
+            dma((every,)),
+            dma((layers,)),
+            dma((layers,)),
+            dma((layers,)),
+            dma((2,)),
         ],
         compiler_params=pltpu.CompilerParams(
             collective_id=3,
             has_side_effects=True,
-            vmem_limit_bytes=62 * 1024 * 1024,
+            vmem_limit_bytes=46 * 1024 * 1024,
         ),
         name="net",
-    )((in_block % cb).reshape(-1), features, tiles, biases)
+    )(in_block.transpose(2, 0, 1), features, tiles, biases)
     return acts, row_means[0], grand[0, 0]
 
 

time: 288 us -> 266 us (0.924)
  Pallas kernels: 278 us -> 258 us
    pallas_call x1, Pallas kernels: 278 us -> 258 us  [fused(): pl.pallas_call(functools.partial(fused_kernel, geo, pieces, cb * side * s...]
    unnamed x1 -> x8, local copies, waits for them, and re-layouts: 4.57 us -> 6.02 us
where the time goes in v2:
time: 266 us
  Pallas kernels  258 us (97%)
  local copies, waits for them, and re-layouts  6.02 us (2%)
    pallas_call x1, Pallas kernels, fused(): pl.pallas_call(functools.partial(fused_kernel, geo, pieces, cb * side * s...  258 us
    unnamed x8, local copies, waits for them, and re-layouts  6.02 us

profile of v2, /device:TPU:0, one launch (start us, length us, event | category | flops | bytes accessed | tf_op | source)
XLA Modules:
  0.0 266.2 jit_solution(16798618428390023234)
XLA Ops:
  0.6 0.0 copy-start
  0.6 1.9 copy-done
  2.5 0.0 copy-start.1
  2.5 0.9 copy-done.1
  3.4 0.0 copy-start.2
  3.4 0.7 copy-done.2
  4.1 257.8 %net.1 = (bf16[128,16384]{1,0:T(8,128)(2,1)S(1)}, f32[1,128]{1,0:T(1,128)S(1)}, f32[1,1]{1,0:T(1,128)}) custom-call(s32[3,2,512]{2,1,0:T(2,128)S(1)} %bitcast.3, bf16[128,16384]{1,0:T(8,128)(2,1)} %feats.1, bf16[2,128,3,16,128]{4,3,2,1,0:T(8,128)(2,1)S(1)} %copy-done, f32[2,16384]{1,0:T(2,128)S(1)} %copy-done.1), custom_call_target="tpu_custom_call" | custom-call | tf_op jit(solution)/shard_map/net/pallas_call | solution.py:866
  261.9 2.0 copy.10
  263.9 0.5 copy.11
Async XLA Ops:
  0.6 1.9 copy-start
  2.5 0.9 copy-start.1
  3.4 0.7 copy-start.2

commit v3 on v0

--- a/solution.py
+++ b/solution.py
@@ -9,6 +9,7 @@
 from jax.sharding import PartitionSpec as P
 
 MESH = pl.DeviceIdType.MESH
+PIECES = 4
 
 
 def geometry(mesh):
@@ -401,6 +402,582 @@
     return mine[0], whole[0]
 
 
+def fused_kernel(
+    geo, pieces, neurons, total_rows,
+    ids, feats, tiles, biases, out, rows_ref, grand_ref,
+    wl, bl, xin, x2, x2g, st, fin, fing, sums, guests, line, slots,
+    lsem, qsend, qrecv, bsem, up, dn, xs, wrecv, xrecv, rrecv,
+    osend, okept, orecv, x2recv, fsem, gsend, msem,
+):
+    nl, nq, line_major, nc = geo
+    layers, groups, shards, per, fan, _, side = wl.shape
+    ny = shards // nc
+    cb = per * shards
+    n = per // pieces
+    chunks = shards * pieces
+    every = layers * chunks
+    shared = chunks + pieces
+    depth = nl
+    bi = lax.axis_index("batch")
+    mi = lax.axis_index("mp")
+    if line_major:
+        l, q = bi // nq, bi % nq
+    else:
+        l, q = bi % nl, bi // nl
+    y, core = mi // nc, mi % nc
+    side_q = (q + 1) % nq
+    total = groups * shards
+    me = bi * shards + mi
+    edge = (l == 0) | (l == nl - 1)
+    host = (l == 1) | (l == nl - 2)
+    low = l < nl // 2
+
+    def group(level, column):
+        return level * nq + column if line_major else column * nl + level
+
+    upper = group(jnp.minimum(l + 1, nl - 1), q)
+    under = group(jnp.maximum(l - 1, 0), q)
+    beside = group(l, side_q)
+    hosted = group(jnp.where(low, 0, nl - 1), q)
+    hosting = group(jnp.where(low, 1, nl - 2), q)
+
+    def source(k):
+        return ((y + k // nc) % ny) * nc + (core + k % nc) % nc
+
+    def turn(layer, c):
+        k = c // pieces
+        return jnp.where(layer == layers - 1, shards - 1 - k, k)
+
+    def spot(p):
+        c = p % chunks
+        return p // chunks, turn(p // chunks, c), c % pieces
+
+    def peer(d):
+        to = (me + d) % total
+        return to // shards, to % shards
+
+    def remote(src, dst, ssem, rsem, b, m):
+        return pltpu.make_async_remote_copy(
+            src_ref=src, dst_ref=dst, send_sem=ssem, recv_sem=rsem,
+            device_id=(b, m), device_id_type=MESH,
+        )
+
+    def came(part, rsem):
+        remote(part, part, msem.at[0], rsem, bi, mi).wait_recv()
+
+    def left(part, ssem):
+        remote(part, part, ssem, msem.at[1], bi, mi).wait_send()
+
+    def own_quarter(layer):
+        return pltpu.make_async_copy(
+            tiles.at[layer, pl.ds(mi * per, per)], wl.at[layer, bi, mi], lsem.at[2 + layer]
+        )
+
+    for layer in range(layers):
+        own_quarter(layer).start()
+    mine_b = pl.ds(mi * per * side, per * side)
+    in_b = pltpu.make_async_copy(biases.at[:, mine_b], bl.at[:, mine_b], lsem.at[1])
+    in_b.start()
+
+    barrier = pltpu.get_barrier_semaphore()
+
+    def greet(b, m):
+        pl.semaphore_signal(barrier, inc=1, device_id=(b, m), device_id_type=MESH)
+
+    @pl.when(l > 0)
+    def _():
+        greet(under, mi)
+
+    @pl.when(l < nl - 1)
+    def _():
+        greet(upper, mi)
+
+    greet(beside, mi)
+    for k in range(1, shards):
+        greet(bi, source(k))
+
+    @pl.loop(0, cb)
+    def _(j):
+        pltpu.make_async_copy(
+            feats.at[:, pl.ds(j * side, side)], xin.at[j], lsem.at[0]
+        ).start()
+
+    near = jnp.where(l > 0, 1, 0) + jnp.where(l < nl - 1, 1, 0)
+    pl.semaphore_wait(barrier, near + shards)
+
+    def quarter(layer, k):
+        to = source(k)
+        return remote(
+            tiles.at[layer, pl.ds(to * per, per)], wl.at[layer, bi, mi],
+            qsend, qrecv.at[layer, mi], bi, to,
+        )
+
+    for k in range(1, shards):
+        to = source(k)
+        quarter(0, k).start()
+        theirs = biases.at[:, pl.ds(to * per * side, per * side)]
+        remote(theirs, bl.at[:, mine_b], bsem.at[0], bsem.at[1], bi, to).start()
+    for layer in range(1, layers):
+        for k in range(1, shards):
+            quarter(layer, k).start()
+    sums[...] = jnp.zeros_like(sums)
+    guests[...] = jnp.zeros_like(guests)
+
+    def piece(p, b):
+        layer, k, g = spot(p)
+        return wl.at[layer, b, source(k), pl.ds(g * n, n)]
+
+    def inside(p):
+        return p >= shared
+
+    def top(p):
+        return jnp.where(inside(p), nl - 2, nl - 1)
+
+    def bottom(p):
+        return jnp.where(inside(p), 1, 0)
+
+    def relayed(p, level):
+        outer = (level == 0) | (level == nl - 1)
+        return (outer & inside(p)) | (jnp.logical_not(outer) & (p % 2 == 1))
+
+    def go(cond, copy):
+        @pl.when(cond)
+        def _():
+            copy.start()
+
+    def along(p, b, level, e):
+        part = piece(p, b)
+        go(l < top(p), remote(part, part, up.at[e], wrecv.at[level, p], upper, mi))
+        go(l > bottom(p), remote(part, part, dn.at[e], wrecv.at[level, p], under, mi))
+
+    def flow(t):
+        @pl.when(t < every)
+        def _():
+            layer, k, g = spot(t)
+
+            @pl.when((g == 0) & (k == 0))
+            def _():
+                own_quarter(layer).wait()
+
+            @pl.when((g == 0) & (k > 0))
+            def _():
+                m = source(k)
+                came(wl.at[layer, bi, m], qrecv.at[layer, m])
+
+            part = piece(t, bi)
+            again = relayed(t, l)
+            go(l < top(t), remote(part, part, up.at[0], wrecv.at[l, t], upper, mi))
+            go(l > bottom(t), remote(part, part, dn.at[0], wrecv.at[l, t], under, mi))
+            go(again, remote(part, part, xs.at[l], rrecv.at[t], beside, mi))
+            go(jnp.logical_not(again), remote(part, part, xs.at[l], xrecv.at[t], beside, mi))
+
+        for d in range(1, nl):
+            p = t - d
+            ok = (p >= 0) & (p < every)
+
+            def step(p, level, onward, ssem, to):
+                part = piece(p, group(level, q))
+                came(part, wrecv.at[level, p])
+                go(onward, remote(part, part, ssem, wrecv.at[level, p], to, mi))
+                direct = jnp.logical_not((abs(level - l) == 1) & relayed(p, level))
+                go(direct, remote(part, part, xs.at[level], xrecv.at[p], beside, mi))
+
+            @pl.when(ok & (l - d >= 0) & (l <= top(p)))
+            def _(d=d, p=p, step=step):
+                step(p, jnp.maximum(l - d, 0), l < top(p), up.at[d], upper)
+
+            @pl.when(ok & (l + d <= nl - 1) & (l >= bottom(p)))
+            def _(d=d, p=p, step=step):
+                step(p, jnp.minimum(l + d, nl - 1), l > bottom(p), dn.at[d], under)
+
+            if d == 1:
+                @pl.when(ok & relayed(p, l))
+                def _(p=p):
+                    part = piece(p, beside)
+                    came(part, rrecv.at[p])
+                    go(l < top(p), remote(part, part, up.at[nl], xrecv.at[p], upper, mi))
+                    go(l > bottom(p), remote(part, part, dn.at[nl], xrecv.at[p], under, mi))
+
+    def landing(p):
+        layer, k, g = spot(p)
+        early = relayed(p, l)
+
+        def wait(count):
+            came(wl.at[layer, pl.ds(0, count), source(k), pl.ds(g * n, n)], xrecv.at[p])
+
+        @pl.when(early)
+        def _():
+            wait(nl - 1)
+
+        @pl.when(jnp.logical_not(early))
+        def _():
+            wait(nl)
+
+    def columns(m, g):
+        return pl.ds((m * per + g * n) * side, n * side)
+
+    def blocks(m, g):
+        return pl.ds(m * per + g * n, n)
+
+    def hand_on(p):
+        c, k, g = p, turn(0, p), p % pieces
+        first = p < chunks
+
+        @pl.when(first & (k == 0))
+        def _():
+            pltpu.make_async_copy(
+                st.at[0, pl.ds(g * n, n)], x2.at[blocks(mi, g)], okept.at[0]
+            ).start()
+
+        @pl.when(first & (k > 0))
+        def _():
+            remote(
+                st.at[k, pl.ds(g * n, n)], x2.at[blocks(mi, g)],
+                osend.at[0], x2recv.at[c], bi, source(k),
+            ).start()
+
+        @pl.when(jnp.logical_not(first))
+        def _():
+            k, g = turn(1, p - chunks), (p - chunks) % pieces
+            here = jnp.logical_not(edge & inside(p))
+            there = pl.ds(g * n * side, n * side)
+
+            @pl.when(here & (k == 0))
+            def _():
+                pltpu.make_async_copy(
+                    fin.at[0, :, there], out.at[:, columns(mi, g)], okept.at[1]
+                ).start()
+
+            @pl.when(here & (k > 0))
+            def _():
+                remote(
+                    fin.at[k, :, there], out.at[:, columns(mi, g)],
+                    osend.at[1], orecv, bi, source(k),
+                ).start()
+
+            @pl.when(host & inside(p))
+            def _():
+                remote(
+                    fing.at[k, :, there], out.at[:, columns(mi, g)],
+                    gsend, orecv, hosted, source(k),
+                ).start()
+
+    def pass_on(c):
+        k, g = turn(0, c), c % pieces
+        m = source(k)
+
+        @pl.when(k == 0)
+        def _():
+            part = st.at[0, pl.ds(g * n, n)]
+            go(edge, remote(part, x2g.at[blocks(mi, g)], fsem.at[0], fsem.at[1], hosting, mi))
+
+        @pl.when(k > 0)
+        def _():
+            part = x2.at[blocks(m, g)]
+            came(part, x2recv.at[c])
+            go(edge, remote(part, x2g.at[blocks(m, g)], fsem.at[0], fsem.at[1], hosting, mi))
+
+    def compute(layer, c, guest=False):
+        k, g = turn(layer, c), c % pieces
+        m = source(k)
+        src = xin if layer == 0 else x2g if guest else x2
+        for jj in range(n):
+            j = g * n + jj
+            column = m * cb + mi * per + j
+            xparts, wparts = [], []
+            for t in range(fan):
+                at = lax.rem(ids[t, layer, column], cb)
+                xparts.append(src[at])
+                wparts.append(wl[layer, :, m, j, t].reshape(side, side))
+            whole = jnp.dot(
+                jnp.concatenate(xparts, axis=1),
+                jnp.concatenate(wparts, axis=0),
+                preferred_element_type=jnp.float32,
+            )
+            bias = bl[layer : layer + 1, pl.ds(pl.multiple_of((m * per + j) * side, side), side)]
+            res = jnp.clip(whole + bias, 0.0, 32.0).astype(out.dtype)
+            cols = pl.ds(pl.multiple_of(j * side, side), side)
+            if layer == 0:
+                st[k, j] = res
+            elif guest:
+                fing[k, :, cols] = res
+                guests[...] += res.astype(jnp.float32)
+            else:
+                fin[k, :, cols] = res
+                sums[...] += res.astype(jnp.float32)
+
+    lag = 2
+
+    @pl.loop(0, every + depth + 1)
+    def _(t):
+        flow(t)
+        p = t - depth
+
+        @pl.when(p >= 1)
+        def _():
+            hand_on(p - 1)
+
+        @pl.when((p >= lag) & (p - lag < chunks - 1))
+        def _():
+            pass_on(p - lag)
+
+        @pl.when(p == 0)
+        def _():
+            pltpu.make_async_copy(xin, xin, lsem.at[0]).wait()
+            in_b.wait()
+            came(bl.at[:, pl.ds(0, (shards - 1) * per * side)], bsem.at[1])
+
+        @pl.when((p >= 0) & (p < chunks))
+        def _():
+            landing(p)
+            compute(0, p)
+
+        @pl.when(p == chunks)
+        def _():
+            pass_on(chunks - 1)
+            pltpu.make_async_copy(st.at[0], st.at[0], okept.at[0]).wait()
+
+        @pl.when((p == shared) & host)
+        def _():
+            came(x2g, fsem.at[1])
+
+        @pl.when((p >= chunks) & (p < every) & jnp.logical_not(edge & inside(p)))
+        def _():
+            landing(p)
+
+        @pl.when((p >= shared) & (p < every) & host)
+        def _():
+            compute(1, p - chunks, True)
+
+        @pl.when((p >= chunks) & (p < every) & jnp.logical_not(edge & inside(p)))
+        def _():
+            compute(1, p - chunks)
+
+    own_line = jnp.sum(sums[...].T, axis=0, keepdims=True)
+    guest_line = jnp.sum(guests[...].T, axis=0, keepdims=True)
+    at_row = lax.broadcasted_iota(jnp.int32, line.shape, 0)
+    line[...] = jnp.where(at_row < line.shape[0] // 2, own_line, guest_line)
+
+    def gone(halves, ssem):
+        if halves % 2 == 0:
+            left(wl.at[0, pl.ds(0, halves // 2), 0], ssem)
+        else:
+            left(wl.at[0, pl.ds(0, halves), 0, pl.ds(0, per // 2)], ssem)
+
+    wide, narrow = 2 * (shards + 1), 2 * (shards - 1)
+    full = wide + narrow
+    for d in range(nl):
+        @pl.when((l - d >= 0) & (l < nl - 2))
+        def _(d=d):
+            gone(full, up.at[d])
+
+        @pl.when((l - d >= 0) & (l == nl - 2))
+        def _(d=d):
+            gone(wide, up.at[d])
+
+        @pl.when((l + d <= nl - 1) & (l > 1))
+        def _(d=d):
+            gone(full, dn.at[d])
+
+        @pl.when((l + d <= nl - 1) & (l == 1))
+        def _(d=d):
+            gone(wide, dn.at[d])
+
+    @pl.when(l == 0)
+    def _():
+        gone(narrow, up.at[nl])
+
+    @pl.when((l > 0) & (l < nl - 2))
+    def _():
+        gone(full // 2, up.at[nl])
+
+    @pl.when(l == nl - 2)
+    def _():
+        gone(wide // 2, up.at[nl])
+
+    @pl.when(l == nl - 1)
+    def _():
+        gone(narrow, dn.at[nl])
+
+    @pl.when((l > 1) & (l < nl - 1))
+    def _():
+        gone(full // 2, dn.at[nl])
+
+    @pl.when(l == 1)
+    def _():
+        gone(wide // 2, dn.at[nl])
+
+    for level in range(nl):
+        close = abs(l - level) == 1
+        outer = level in (0, nl - 1)
+
+        @pl.when(l == level)
+        def _(level=level):
+            gone(full, xs.at[level])
+
+        @pl.when(edge & (l != level))
+        def _(level=level, close=close):
+            @pl.when(close)
+            def _():
+                gone(wide // 2, xs.at[level])
+
+            @pl.when(jnp.logical_not(close))
+            def _():
+                gone(wide, xs.at[level])
+
+        @pl.when(jnp.logical_not(edge) & (l != level))
+        def _(level=level, close=close, outer=outer):
+            @pl.when(close)
+            def _():
+                gone(wide if outer else full // 2, xs.at[level])
+
+            @pl.when(jnp.logical_not(close))
+            def _():
+                gone(full, xs.at[level])
+
+    left(wl.at[:, bi, pl.ds(0, shards - 1)], qsend)
+    left(bl.at[:, pl.ds(0, (shards - 1) * per * side)], bsem.at[0])
+    left(st.at[pl.ds(0, shards - 1)], osend.at[0])
+
+    @pl.when(edge)
+    def _():
+        left(x2g, fsem.at[0])
+
+    def mcopy(d, slot):
+        return remote(line, slots.at[slot], msem.at[0], msem.at[1], *peer(d))
+
+    @pl.loop(1, total)
+    def _(d):
+        mcopy(d, me).start()
+
+    slots[me] = line[...]
+
+    @pl.when(edge)
+    def _():
+        left(fin.at[0], osend.at[1])
+
+    @pl.when(jnp.logical_not(edge))
+    def _():
+        left(fin.at[pl.ds(0, shards - 1)], osend.at[1])
+
+    @pl.when(host)
+    def _():
+        left(fing, gsend)
+
+    lines = slots.at[pl.ds(0, total - 1)]
+    came(lines, msem.at[1])
+    low_half = line.shape[0] // 2
+    whole = jnp.zeros((1, line.shape[1]), jnp.float32)
+    for b in range(groups):
+        one = slots[b * shards]
+        for m in range(1, shards):
+            one = one + slots[b * shards + m]
+        whole = whole + (one[0:1] + one[low_half : low_half + 1]) / neurons
+    mine = slots[bi * shards]
+    help_ = slots[hosting * shards]
+    for m in range(1, shards):
+        mine = mine + slots[bi * shards + m]
+        help_ = help_ + slots[hosting * shards + m]
+    extra = jnp.where(edge, help_[low_half : low_half + 1], 0.0)
+    rows_ref[...] = (mine[0:1] + extra) / neurons
+    grand_ref[0, 0] = jnp.sum(whole) / total_rows
+
+    @pl.when(edge)
+    def _():
+        came(fin, orecv)
+
+    @pl.when(jnp.logical_not(edge))
+    def _():
+        pltpu.make_async_copy(fin.at[0], fin.at[0], okept.at[1]).wait()
+        came(fin.at[pl.ds(0, shards - 1)], orecv)
+
+    left(lines, msem.at[0])
+
+
+def fused(geo, pieces, features, tiles, biases, in_block):
+    nl, nq, _, nc = geo
+    shards = lax.axis_size("mp")
+    groups = lax.axis_size("batch")
+    layers, cb, fan, depth, side = tiles.shape
+    rows, width = features.shape
+    per = cb // shards
+    chunks = shards * pieces
+    every = layers * chunks
+    total = groups * shards
+    dma = pltpu.SemaphoreType.DMA
+    hbm = pl.BlockSpec(memory_space=pltpu.HBM)
+    vmem = pl.BlockSpec(memory_space=pltpu.VMEM)
+    smem = pl.BlockSpec(memory_space=pltpu.SMEM)
+    blocks = pltpu.VMEM((cb, rows, side), features.dtype)
+    sums = pltpu.VMEM((rows, side), jnp.float32)
+    acts, row_means, grand = pl.pallas_call(
+        functools.partial(
+            fused_kernel, geo, pieces, cb * side * shards, rows * groups
+        ),
+        out_shape=(
+            jax.ShapeDtypeStruct((rows, width), features.dtype),
+            jax.ShapeDtypeStruct((1, rows), jnp.float32),
+            jax.ShapeDtypeStruct((1, 1), jnp.float32),
+        ),
+        in_specs=[smem, hbm, hbm, hbm],
+        out_specs=(pl.BlockSpec(memory_space=pl.ANY), vmem, smem),
+        scratch_shapes=[
+            pltpu.VMEM((layers, groups, shards, per, fan, depth, side), tiles.dtype),
+            pltpu.VMEM(biases.shape, biases.dtype),
+            blocks,
+            blocks,
+            blocks,
+            pltpu.VMEM((shards, per, rows, side), features.dtype),
+            pltpu.VMEM((shards, rows, per * side), features.dtype),
+            pltpu.VMEM((shards - 1, rows, per * side), features.dtype),
+            sums,
+            sums,
+            pltpu.VMEM((8, rows), jnp.float32),
+            pltpu.VMEM((total, 8, rows), jnp.float32),
+            dma((2 + layers,)),
+            dma(()),
+            dma((layers, shards)),
+            dma((2,)),
+            dma((nl + 1,)),
+            dma((nl + 1,)),
+            dma((nl,)),
+            dma((nl, every)),
+            dma((every,)),
+            dma((every,)),
+            dma((2,)),
+            dma((2,)),
+            dma(()),
+            dma((chunks,)),
+            dma((2,)),
+            dma(()),
+            dma((2,)),
+        ],
+        compiler_params=pltpu.CompilerParams(
+            collective_id=3,
+            has_side_effects=True,
+            vmem_limit_bytes=54 * 1024 * 1024,
+        ),
+        name="net",
+    )(in_block.transpose(2, 0, 1), features, tiles, biases)
+    return acts, row_means[0], grand[0, 0]
+
+
+def suits(geo, shards, groups, features, tiles, biases):
+    nl, nq, _, nc = geo
+    kept = 6 * features.size + groups * tiles.size
+    return (
+        nq == 2
+        and nl == 4
+        and nc <= 2
+        and shards == 2 * nc
+        and groups >= 2 * shards
+        and tiles.shape[0] == 2
+        and tiles.shape[3] % 16 == 0
+        and tiles.shape[1] // shards % PIECES == 0
+        and 2 * kept < 54 * 1024 * 1024
+    )
+
+
 def on_device(geo, features, tiles, biases, in_block):
     shards = lax.axis_size("mp")
     groups = lax.axis_size("batch")
@@ -409,6 +986,8 @@
     side = tiles.shape[4]
     cb = tiles.shape[1]
     fan = tiles.shape[2]
+    if suits(geo, shards, groups, features, tiles, biases):
+        return fused(geo, PIECES, features, tiles, biases, in_block)
     current = features
     mine = lax.dynamic_slice_in_dim(in_block, me * cb, cb, axis=1) % cb
     for layer in range(tiles.shape[0]):

time: 308 us -> 263 us (0.85)
  Pallas kernels: 299 us -> 255 us
    pallas_call x5 -> x1, Pallas kernels: 299 us -> 255 us  [fused(): pl.pallas_call(functools.partial(fused_kernel, geo, pieces, cb * side * s...]
    unnamed x2 -> x4, local copies, waits for them, and re-layouts: 0.59 us -> 5.09 us
where the time goes in v3:
time: 263 us
  Pallas kernels  255 us (97%)
  local copies, waits for them, and re-layouts  5.09 us (2%)
    pallas_call x1, Pallas kernels, fused(): pl.pallas_call(functools.partial(fused_kernel, geo, pieces, cb * side * s...  255 us

profile of v3, /device:TPU:0, one launch (start us, length us, event | category | flops | bytes accessed | tf_op | source)
XLA Modules:
  0.0 262.9 jit_solution(7752484372119931948)
XLA Ops:
  0.6 255.5 %net.1 = (bf16[128,16384]{1,0:T(8,128)(2,1)}, f32[1,128]{1,0:T(1,128)}, f32[1,1]{1,0:T(1,128)}) custom-call(s32[3,2,512]{2,1,0:T(2,128)} %bitcast.3, bf16[128,16384]{1,0:T(8,128)(2,1)} %feats.1, bf16[2,128,3,16,128]{4,3,2,1,0:T(8,128)(2,1)} %tiles.1, f32[2,16384]{1,0:T(2,128)} %biases.1), custom_call_target="tpu_custom_call" | custom-call | tf_op jit(solution)/shard_map/net/pallas_call | solution.py:913
  256.1 0.0 copy-start
  256.1 4.6 %copy.10 = bf16[128,16384]{1,0:T(8,128)(2,1)} copy(bf16[128,16384]{1,0:T(8,128)(2,1)} %get-tuple-element.12) | data formatting | bytes 8388608
  260.7 0.0 copy-done
  260.7 0.5 copy.11
Async XLA Ops:
  256.1 4.6 %copy-start = (f32[1,128]{1,0:T(1,128)S(1)}, f32[1,128]{1,0:T(1,128)}, u32[]{:S(2)}) copy-start(f32[1,128]{1,0:T(1,128)} %get-tuple-element.7) | copy-start | bytes 1540

commit v4 on v3

--- a/solution.py
+++ b/solution.py
@@ -10,6 +10,11 @@
 
 MESH = pl.DeviceIdType.MESH
 PIECES = 4
+KEPT = 2
+FIRST = 2
+LAG = 1
+LATER = 0
+SLACK = 2
 
 
 def geometry(mesh):
@@ -416,8 +421,8 @@
     n = per // pieces
     chunks = shards * pieces
     every = layers * chunks
-    shared = chunks + pieces
     depth = nl
+    edge_own = KEPT * pieces
     bi = lax.axis_index("batch")
     mi = lax.axis_index("mp")
     if line_major:
@@ -446,11 +451,19 @@
 
     def turn(layer, c):
         k = c // pieces
-        return jnp.where(layer == layers - 1, shards - 1 - k, k)
+        return (shards - k) % shards if layer == 0 else shards - 1 - k
+
+    def place(p):
+        r = p - chunks
+        v = r - FIRST
+        mixed = jnp.where(v % 2 == 1, FIRST + v // 2, edge_own + v // 2)
+        later = jnp.where(v < 2 * (edge_own - FIRST), mixed, r)
+        second = jnp.where(r < FIRST, r, later)
+        return jnp.where(r >= 0, 1, 0), jnp.where(r >= 0, second, p)
 
     def spot(p):
-        c = p % chunks
-        return p // chunks, turn(p // chunks, c), c % pieces
+        layer, c = place(p)
+        return layer, jnp.where(layer == 0, turn(0, c), turn(1, c)), c % pieces
 
     def peer(d):
         to = (me + d) % total
@@ -528,7 +541,8 @@
         return wl.at[layer, b, source(k), pl.ds(g * n, n)]
 
     def inside(p):
-        return p >= shared
+        layer, c = place(p)
+        return (layer == 1) & (c >= edge_own)
 
     def top(p):
         return jnp.where(inside(p), nl - 2, nl - 1)
@@ -538,7 +552,12 @@
 
     def relayed(p, level):
         outer = (level == 0) | (level == nl - 1)
-        return (outer & inside(p)) | (jnp.logical_not(outer) & (p % 2 == 1))
+        return jnp.where(outer, p >= chunks, place(p)[1] % 2 == 1)
+
+    def carried(p, level, to):
+        outer = (to == 0) | (to == nl - 1)
+        across = (abs(level - to) == 1) & relayed(p, level)
+        return across & jnp.logical_not(outer & (p >= chunks))
 
     def go(cond, copy):
         @pl.when(cond)
@@ -550,10 +569,14 @@
         go(l < top(p), remote(part, part, up.at[e], wrecv.at[level, p], upper, mi))
         go(l > bottom(p), remote(part, part, dn.at[e], wrecv.at[level, p], under, mi))
 
+    def due(t, d):
+        one, two = t - d, t - d - SLACK
+        ok = ((one >= 0) & (one < chunks)) | ((two >= chunks) & (two < every))
+        return jnp.where(one < chunks, one, two), ok
+
     def flow(t):
-        @pl.when(t < every)
-        def _():
-            layer, k, g = spot(t)
+        def quarter_here(p):
+            layer, k, g = spot(p)
 
             @pl.when((g == 0) & (k == 0))
             def _():
@@ -564,22 +587,43 @@
                 m = source(k)
                 came(wl.at[layer, bi, m], qrecv.at[layer, m])
 
+        def own(p, cond):
+            part = piece(p, bi)
+            go(cond & (l < top(p)), remote(part, part, up.at[0], wrecv.at[l, p], upper, mi))
+            go(cond & (l > bottom(p)), remote(part, part, dn.at[0], wrecv.at[l, p], under, mi))
+
+        hurried = pieces + 2 * (t - pieces)
+
+        @pl.when((t < pieces) | ((t >= chunks) & (t < every)))
+        def _():
+            quarter_here(t)
+            own(t, True)
+
+        @pl.when((t >= pieces) & (hurried < chunks))
+        def _():
+            quarter_here(hurried)
+            own(hurried, edge)
+            own(hurried + 1, edge)
+
+        @pl.when((t >= pieces) & (t < chunks))
+        def _():
+            own(t, jnp.logical_not(edge))
+
+        @pl.when(t < every)
+        def _():
             part = piece(t, bi)
             again = relayed(t, l)
-            go(l < top(t), remote(part, part, up.at[0], wrecv.at[l, t], upper, mi))
-            go(l > bottom(t), remote(part, part, dn.at[0], wrecv.at[l, t], under, mi))
             go(again, remote(part, part, xs.at[l], rrecv.at[t], beside, mi))
             go(jnp.logical_not(again), remote(part, part, xs.at[l], xrecv.at[t], beside, mi))
 
         for d in range(1, nl):
-            p = t - d
-            ok = (p >= 0) & (p < every)
+            p, ok = due(t, d)
 
             def step(p, level, onward, ssem, to):
                 part = piece(p, group(level, q))
                 came(part, wrecv.at[level, p])
                 go(onward, remote(part, part, ssem, wrecv.at[level, p], to, mi))
-                direct = jnp.logical_not((abs(level - l) == 1) & relayed(p, level))
+                direct = jnp.logical_not(carried(p, level, l))
                 go(direct, remote(part, part, xs.at[level], xrecv.at[p], beside, mi))
 
             @pl.when(ok & (l - d >= 0) & (l <= top(p)))
@@ -595,8 +639,10 @@
                 def _(p=p):
                     part = piece(p, beside)
                     came(part, rrecv.at[p])
-                    go(l < top(p), remote(part, part, up.at[nl], xrecv.at[p], upper, mi))
-                    go(l > bottom(p), remote(part, part, dn.at[nl], xrecv.at[p], under, mi))
+                    more = (l < top(p)) & carried(p, l, l + 1)
+                    go(more, remote(part, part, up.at[nl], xrecv.at[p], upper, mi))
+                    more = (l > bottom(p)) & carried(p, l, l - 1)
+                    go(more, remote(part, part, dn.at[nl], xrecv.at[p], under, mi))
 
     def landing(p):
         layer, k, g = spot(p)
@@ -620,47 +666,52 @@
         return pl.ds(m * per + g * n, n)
 
     def hand_on(p):
-        c, k, g = p, turn(0, p), p % pieces
-        first = p < chunks
-
-        @pl.when(first & (k == 0))
-        def _():
-            pltpu.make_async_copy(
-                st.at[0, pl.ds(g * n, n)], x2.at[blocks(mi, g)], okept.at[0]
-            ).start()
-
-        @pl.when(first & (k > 0))
-        def _():
-            remote(
-                st.at[k, pl.ds(g * n, n)], x2.at[blocks(mi, g)],
-                osend.at[0], x2recv.at[c], bi, source(k),
-            ).start()
-
-        @pl.when(jnp.logical_not(first))
-        def _():
-            k, g = turn(1, p - chunks), (p - chunks) % pieces
-            here = jnp.logical_not(edge & inside(p))
-            there = pl.ds(g * n * side, n * side)
-
-            @pl.when(here & (k == 0))
+        layer, c = place(p)
+        g = c % pieces
+
+        @pl.when(layer == 0)
+        def _():
+            k = turn(0, c)
+            part = pl.ds(g * n, n)
+
+            @pl.when(k == 0)
             def _():
                 pltpu.make_async_copy(
-                    fin.at[0, :, there], out.at[:, columns(mi, g)], okept.at[1]
+                    st.at[0, part], x2.at[blocks(mi, g)], okept.at[0]
                 ).start()
 
-            @pl.when(here & (k > 0))
+            @pl.when(k > 0)
             def _():
                 remote(
-                    fin.at[k, :, there], out.at[:, columns(mi, g)],
+                    st.at[k, part], x2.at[blocks(mi, g)],
+                    osend.at[0], x2recv.at[c], bi, source(k),
+                ).start()
+
+        @pl.when((layer == 1) & jnp.logical_not(edge & inside(p)))
+        def _():
+            k = turn(1, c)
+            part = pl.ds(g * n * side, n * side)
+
+            @pl.when(k == 0)
+            def _():
+                pltpu.make_async_copy(
+                    fin.at[0, :, part], out.at[:, columns(mi, g)], okept.at[1]
+                ).start()
+
+            @pl.when(k > 0)
+            def _():
+                remote(
+                    fin.at[k, :, part], out.at[:, columns(mi, g)],
                     osend.at[1], orecv, bi, source(k),
                 ).start()
 
-            @pl.when(host & inside(p))
-            def _():
-                remote(
-                    fing.at[k, :, there], out.at[:, columns(mi, g)],
-                    gsend, orecv, hosted, source(k),
-                ).start()
+    def give_back(p):
+        _, c = place(p)
+        k, g = turn(1, c), c % pieces
+        remote(
+            fing.at[k, :, pl.ds(g * n * side, n * side)], out.at[:, columns(mi, g)],
+            gsend, orecv, hosted, source(k),
+        ).start()
 
     def pass_on(c):
         k, g = turn(0, c), c % pieces
@@ -706,20 +757,28 @@
                 fin[k, :, cols] = res
                 sums[...] += res.astype(jnp.float32)
 
-    lag = 2
-
-    @pl.loop(0, every + depth + 1)
+    @pl.loop(0, every + depth + SLACK + LATER + 1)
     def _(t):
         flow(t)
         p = t - depth
-
-        @pl.when(p >= 1)
+        r = p - SLACK
+        h = r - LATER
+
+        @pl.when((p >= 1) & (p <= chunks))
         def _():
             hand_on(p - 1)
 
-        @pl.when((p >= lag) & (p - lag < chunks - 1))
-        def _():
-            pass_on(p - lag)
+        @pl.when((r > chunks) & (r <= every))
+        def _():
+            hand_on(r - 1)
+
+        @pl.when(host & (h > chunks))
+        def _():
+            pl.when(inside(h - 1))(lambda: give_back(h - 1))
+
+        @pl.when((p >= LAG) & (p - LAG < chunks))
+        def _():
+            pass_on(p - LAG)
 
         @pl.when(p == 0)
         def _():
@@ -732,26 +791,27 @@
             landing(p)
             compute(0, p)
 
-        @pl.when(p == chunks)
-        def _():
-            pass_on(chunks - 1)
+        @pl.when(r == chunks)
+        def _():
             pltpu.make_async_copy(st.at[0], st.at[0], okept.at[0]).wait()
 
-        @pl.when((p == shared) & host)
+        needed = (r >= chunks) & (r < every) & jnp.logical_not(edge & inside(r))
+
+        @pl.when(needed)
+        def _():
+            landing(r)
+
+        @pl.when(host & (h == chunks + FIRST))
         def _():
             came(x2g, fsem.at[1])
 
-        @pl.when((p >= chunks) & (p < every) & jnp.logical_not(edge & inside(p)))
-        def _():
-            landing(p)
-
-        @pl.when((p >= shared) & (p < every) & host)
-        def _():
-            compute(1, p - chunks, True)
-
-        @pl.when((p >= chunks) & (p < every) & jnp.logical_not(edge & inside(p)))
-        def _():
-            compute(1, p - chunks)
+        @pl.when(host & (h >= chunks) & (h < every))
+        def _():
+            pl.when(inside(h))(lambda: compute(1, place(h)[1], True))
+
+        @pl.when(needed)
+        def _():
+            compute(1, place(r)[1])
 
     own_line = jnp.sum(sums[...].T, axis=0, keepdims=True)
     guest_line = jnp.sum(guests[...].T, axis=0, keepdims=True)
@@ -764,7 +824,7 @@
         else:
             left(wl.at[0, pl.ds(0, halves), 0, pl.ds(0, per // 2)], ssem)
 
-    wide, narrow = 2 * (shards + 1), 2 * (shards - 1)
+    wide, narrow = 2 * (shards + KEPT), 2 * (shards - KEPT)
     full = wide + narrow
     for d in range(nl):
         @pl.when((l - d >= 0) & (l < nl - 2))
@@ -785,7 +845,7 @@
 
     @pl.when(l == 0)
     def _():
-        gone(narrow, up.at[nl])
+        gone(full // 2, up.at[nl])
 
     @pl.when((l > 0) & (l < nl - 2))
     def _():
@@ -793,11 +853,11 @@
 
     @pl.when(l == nl - 2)
     def _():
-        gone(wide // 2, up.at[nl])
+        gone(shards, up.at[nl])
 
     @pl.when(l == nl - 1)
     def _():
-        gone(narrow, dn.at[nl])
+        gone(full // 2, dn.at[nl])
 
     @pl.when((l > 1) & (l < nl - 1))
     def _():
@@ -805,7 +865,7 @@
 
     @pl.when(l == 1)
     def _():
-        gone(wide // 2, dn.at[nl])
+        gone(shards, dn.at[nl])
 
     for level in range(nl):
         close = abs(l - level) == 1
@@ -819,7 +879,7 @@
         def _(level=level, close=close):
             @pl.when(close)
             def _():
-                gone(wide // 2, xs.at[level])
+                gone(wide - shards, xs.at[level])
 
             @pl.when(jnp.logical_not(close))
             def _():
@@ -829,7 +889,7 @@
         def _(level=level, close=close, outer=outer):
             @pl.when(close)
             def _():
-                gone(wide if outer else full // 2, xs.at[level])
+                gone(full // 2, xs.at[level])
 
             @pl.when(jnp.logical_not(close))
             def _():
@@ -854,7 +914,7 @@
 
     @pl.when(edge)
     def _():
-        left(fin.at[0], osend.at[1])
+        left(fin.at[pl.ds(0, KEPT)], osend.at[1])
 
     @pl.when(jnp.logical_not(edge))
     def _():
@@ -929,7 +989,7 @@
             blocks,
             pltpu.VMEM((shards, per, rows, side), features.dtype),
             pltpu.VMEM((shards, rows, per * side), features.dtype),
-            pltpu.VMEM((shards - 1, rows, per * side), features.dtype),
+            pltpu.VMEM((shards - KEPT, rows, per * side), features.dtype),
             sums,
             sums,
             pltpu.VMEM((8, rows), jnp.float32),

time: 263 us -> 257 us (0.977)
  Pallas kernels: 255 us -> 250 us
    pallas_call x1, Pallas kernels: 255 us -> 250 us  [fused(): pl.pallas_call(functools.partial(fused_kernel, geo, pieces, cb * side * s...]
where the time goes in v4:
time: 257 us
  Pallas kernels  250 us (97%)
  local copies, waits for them, and re-layouts  5.09 us (2%)
    pallas_call x1, Pallas kernels, fused(): pl.pallas_call(functools.partial(fused_kernel, geo, pieces, cb * side * s...  250 us

profile of v4, /device:TPU:0, one launch (start us, length us, event | category | flops | bytes accessed | tf_op | source)
XLA Modules:
  0.0 257.0 jit_solution(6572397222395401402)
XLA Ops:
  0.6 249.6 %net.1 = (bf16[128,16384]{1,0:T(8,128)(2,1)}, f32[1,128]{1,0:T(1,128)}, f32[1,1]{1,0:T(1,128)}) custom-call(s32[3,2,512]{2,1,0:T(2,128)} %bitcast.3, bf16[128,16384]{1,0:T(8,128)(2,1)} %feats.1, bf16[2,128,3,16,128]{4,3,2,1,0:T(8,128)(2,1)} %tiles.1, f32[2,16384]{1,0:T(2,128)} %biases.1), custom_call_target="tpu_custom_call" | custom-call | tf_op jit(solution)/shard_map/net/pallas_call | solution.py:973
  250.2 0.0 copy-start
  250.2 4.6 %copy.10 = bf16[128,16384]{1,0:T(8,128)(2,1)} copy(bf16[128,16384]{1,0:T(8,128)(2,1)} %get-tuple-element.12) | data formatting | bytes 8388608
  254.8 0.0 copy-done
  254.8 0.5 copy.11
Async XLA Ops:
  250.2 4.6 %copy-start = (f32[1,128]{1,0:T(1,128)S(1)}, f32[1,128]{1,0:T(1,128)}, u32[]{:S(2)}) copy-start(f32[1,128]{1,0:T(1,128)} %get-tuple-element.7) | copy-start | bytes 1540

commit v5 on v4

--- a/solution.py
+++ b/solution.py
@@ -11,8 +11,8 @@
 MESH = pl.DeviceIdType.MESH
 PIECES = 4
 KEPT = 2
-FIRST = 2
-LAG = 1
+FIRST = 3
+LAG = 2
 LATER = 0
 SLACK = 2
 
@@ -616,6 +616,7 @@
             go(again, remote(part, part, xs.at[l], rrecv.at[t], beside, mi))
             go(jnp.logical_not(again), remote(part, part, xs.at[l], xrecv.at[t], beside, mi))
 
+    def steps(t):
         for d in range(1, nl):
             p, ok = due(t, d)
 
@@ -779,6 +780,8 @@
         @pl.when((p >= LAG) & (p - LAG < chunks))
         def _():
             pass_on(p - LAG)
+
+        steps(t)
 
         @pl.when(p == 0)
         def _():

time: 257 us -> 249 us (0.969)
  Pallas kernels: 250 us -> 241 us
    pallas_call x1, Pallas kernels: 250 us -> 241 us  [fused(): pl.pallas_call(functools.partial(fused_kernel, geo, pieces, cb * side * s...]
where the time goes in v5:
time: 249 us; the launch traced here: 248 us
  Pallas kernels  241 us (97%)
  local copies, waits for them, and re-layouts  5.09 us (2%)
    pallas_call x1, Pallas kernels, fused(): pl.pallas_call(functools.partial(fused_kernel, geo, pieces, cb * side * s...  241 us
    unnamed x4, local copies, waits for them, and re-layouts  5.09 us

profile of v5, /device:TPU:0, one launch (start us, length us, event | category | flops | bytes accessed | tf_op | source)
XLA Modules:
  0.0 248.4 jit_solution(14441466722318666052)
XLA Ops:
  0.6 240.9 %net.1 = (bf16[128,16384]{1,0:T(8,128)(2,1)}, f32[1,128]{1,0:T(1,128)}, f32[1,1]{1,0:T(1,128)}) custom-call(s32[3,2,512]{2,1,0:T(2,128)} %bitcast.3, bf16[128,16384]{1,0:T(8,128)(2,1)} %feats.1, bf16[2,128,3,16,128]{4,3,2,1,0:T(8,128)(2,1)} %tiles.1, f32[2,16384]{1,0:T(2,128)} %biases.1), custom_call_target="tpu_custom_call" | custom-call | tf_op jit(solution)/shard_map/net/pallas_call | solution.py:976
  241.6 0.0 copy-start
  241.6 4.6 %copy.10 = bf16[128,16384]{1,0:T(8,128)(2,1)} copy(bf16[128,16384]{1,0:T(8,128)(2,1)} %get-tuple-element.12) | data formatting | bytes 8388608
  246.1 0.0 copy-done
  246.2 0.5 copy.11
Async XLA Ops:
  241.6 4.6 %copy-start = (f32[1,128]{1,0:T(1,128)S(1)}, f32[1,128]{1,0:T(1,128)}, u32[]{:S(2)}) copy-start(f32[1,128]{1,0:T(1,128)} %get-tuple-element.7) | copy-start | bytes 1540

commit v6 on v5

--- a/solution.py
+++ b/solution.py
@@ -973,6 +973,10 @@
     smem = pl.BlockSpec(memory_space=pltpu.SMEM)
     blocks = pltpu.VMEM((cb, rows, side), features.dtype)
     sums = pltpu.VMEM((rows, side), jnp.float32)
+    kept = [
+        pltpu.with_memory_space_constraint(x, pltpu.HBM)
+        for x in (features, tiles, biases)
+    ]
     acts, row_means, grand = pl.pallas_call(
         functools.partial(
             fused_kernel, geo, pieces, cb * side * shards, rows * groups
@@ -1018,10 +1022,10 @@
         compiler_params=pltpu.CompilerParams(
             collective_id=3,
             has_side_effects=True,
-            vmem_limit_bytes=54 * 1024 * 1024,
+            vmem_limit_bytes=48 * 1024 * 1024,
         ),
         name="net",
-    )(in_block.transpose(2, 0, 1), features, tiles, biases)
+    )(in_block.transpose(2, 0, 1), *kept)
     return acts, row_means[0], grand[0, 0]
 
 

time: 249 us -> 246 us (0.988)
  no operation moved by 1% of the time
where the time goes in v6:
time: 246 us
  Pallas kernels  241 us (98%)
  local copies, waits for them, and re-layouts  3.23 us (1%)
    pallas_call x1, Pallas kernels, fused(): pl.pallas_call(functools.partial(fused_kernel, geo, pieces, cb * side * s...  241 us

profile of v6, /device:TPU:0, one launch (start us, length us, event | category | flops | bytes accessed | tf_op | source)
XLA Modules:
  0.0 246.2 jit_solution(2921629764240565845)
XLA Ops:
  0.6 0.0 copy-start
  0.6 0.7 copy-done
  1.3 240.6 %net.1 = (bf16[128,16384]{1,0:T(8,128)(2,1)S(1)}, f32[1,128]{1,0:T(1,128)S(1)}, f32[1,1]{1,0:T(1,128)}) custom-call(s32[3,2,512]{2,1,0:T(2,128)S(1)} %bitcast.3, bf16[128,16384]{1,0:T(8,128)(2,1)} %feats.1, bf16[2,128,3,16,128]{4,3,2,1,0:T(8,128)(2,1)} %tiles.1, f32[2,16384]{1,0:T(2,128)} %biases.1), custom_call_target="tpu_custom_call" | custom-call | tf_op jit(solution)/shard_map/net/pallas_call | solution.py:980
  241.9 2.0 copy.10
  243.9 0.5 copy.11
Async XLA Ops:
  0.6 0.7 copy-start
